TPU v7x, 128 devices: a whole 4x4x4 slice. The times are simulated.
128 devices in a mesh: rows: 32 (over x, y, core), cores: 4 (over z).
Axes of the slice: x: 4, y: 4, z: 4, core: 2. Of those that a mesh axis runs over, the one named last changes fastest.
Arguments:
- rhs: float32 [524288, 128], P(('rows', 'cores')), may hold values from -6 to 6
- guess: float32 [524288, 128], P(('rows', 'cores')), may hold values from -4 to 4
- degree: float32 [524288], P(('rows', 'cores')), may hold values from 2 to 6
- weights: bfloat16 [4096, 16, 128, 128], P(('rows', 'cores')), may hold values from -0.1875 to 0.1875
- columns: int32 [4096, 16], P(('rows', 'cores')), may hold values from 0 to 287, as said below
- block_counts: int32 [4096], P(('rows', 'cores')), may hold values from 8 to 16, as said below
- send_lists: int32 [128, 128, 2], P(('rows', 'cores')), may hold values from 0 to 31
- aggregates: int32 [524288], P(('rows', 'cores')), may hold values from 0 to 16383
- coarse_diag: float32 [16384], replicated, may hold values from 4 to 32
Outputs:
- smoothed: float32 [524288, 128], P(('rows', 'cores'))
Inputs may be any that keep to these rules, and one draw needn't show every extreme that they name: `block_counts`: every block row has 8 or 16 live slots, and the rows of one device have exactly 320 live slots in all. `columns`: on every device, each table index from 32 up is named by at least one live slot.
All inputs are finite; a program needn't handle non-finite values.
Results may differ from a plain program's by a relative error of at most 0.0022.
Values may be sent and summed in bfloat16 or wider, within the bound.
A program may use at most 128 MiB of HBM per device.

v0:
```python
import jax
import jax.numpy as jnp
from jax import lax
from jax.sharding import PartitionSpec as P

NC = 16384


damping = 0.7


def body(rhs, guess, degree, weights, columns, block_counts, send_lists, aggregates, coarse_diag):
    nblocks = weights.shape[0]
    slots = weights.shape[1]
    blocksize = weights.shape[2]
    width = rhs.shape[1]
    my_lists = send_lists[0]
    flat_live = jnp.arange(slots, dtype=jnp.int32)[None, :] < block_counts[:, None]
    live_weights = weights * flat_live.astype(jnp.bfloat16)[:, :, None, None]

    def apply(field):
        blocks = field.astype(jnp.bfloat16).reshape(nblocks, blocksize, width)
        outgoing = blocks[my_lists]
        incoming = lax.all_to_all(
            outgoing, ("rows", "cores"), split_axis=0, concat_axis=0, tiled=True
        )
        table = jnp.concatenate([blocks, incoming.reshape(-1, blocksize, width)], 0)
        offsum = jnp.einsum(
            "bsij,bsjr->bir", live_weights, table[columns], preferred_element_type=jnp.float32
        )
        return degree[:, None] * field - offsum.reshape(-1, width)

    first = guess + damping * (rhs - apply(guess)) / degree[:, None]
    residue = rhs - apply(first)
    local_coarse = jax.ops.segment_sum(residue, aggregates, num_segments=NC)
    total = lax.psum(local_coarse, ("rows", "cores"))
    correction = (total / coarse_diag[:, None]).astype(jnp.bfloat16)
    second = first + correction[aggregates].astype(jnp.float32)
    return second + damping * (rhs - apply(second)) / degree[:, None]


def solution(mesh):
    return jax.shard_map(
        body,
        mesh=mesh,
        in_specs=(
            P(("rows", "cores"), None),
            P(("rows", "cores"), None),
            P(("rows", "cores")),
            P(("rows", "cores"), None, None, None),
            P(("rows", "cores"), None),
            P(("rows", "cores")),
            P(("rows", "cores"), None, None),
            P(("rows", "cores")),
            P(),
        ),
        out_specs=P(("rows", "cores"), None),
        check_vma=False,
    )
```

profile of v0, /device:TPU:0, one launch (start us, length us, event | category | flops | bytes accessed | tf_op | source)
XLA Modules:
  0.0 700.3 jit_solution(10539362851413579965)
XLA Ops:
  6.5 0.7 compare_select_fusion.2
  7.2 0.1 copy.10
  7.3 0.1 reshape.90
  7.5 1.7 convert_element_type.23
  9.2 8.6 %gather_fusion = bf16[256,128,128]{2,1,0:T(8,128)(2,1)} fusion(bf16[32,128,128]{2,1,0:T(8,128)(2,1)S(1)} %bitcast.53, s32[1024]{0:T(1024)S(1)} %pad_clamp_fusion.1), kind=kCustom, calls=%fused_computation | custom fusion | bytes 16778240 | tf_op jit(solution)/shard_map/gather | solution.py:23
  17.8 0.0 copy-start.8
  17.8 0.0 copy-start.9
  17.8 11.7 %all-to-all-start = ((bf16[128,2,128,128]{3,2,1,0:T(8,128)(2,1)}), bf16[128,2,128,128]{3,2,1,0:T(8,128)(2,1)}, u32[]{:S(2)}, u32[]{:S(2)}) async-start(bf16[128,2,128,128]{3,2,1,0:T(8,128)(2,1)} %bitcast.59), calls=%async_computation | async-start | bytes 16777216 | tf_op jit(solution)/shard_map/all_to_all | solution.py:24
  29.5 0.2 all-reduce.2.cloned.1.call-start
  29.8 0.0 copy-done.8
  29.8 0.1 copy.11
  29.9 0.1 reshape.98
  29.9 0.0 copy-done.9
  30.0 0.1 fusion.22
  30.0 106.8 %all-to-all-done = bf16[128,2,128,128]{3,2,1,0:T(8,128)(2,1)} async-done(((bf16[128,2,128,128]{3,2,1,0:T(8,128)(2,1)}), bf16[128,2,128,128]{3,2,1,0:T(8,128)(2,1)}, u32[]{:S(2)}, u32[]{:S(2)}) %all-to-all-start) | async-done | bytes 8388640 | tf_op jit(solution)/shard_map/all_to_all | solution.py:24
  136.8 7.8 %pad_maximum_fusion = bf16[288,128,128]{2,1,0:T(8,128)(2,1)} fusion(bf16[256,128,128]{2,1,0:T(8,128)(2,1)} %bitcast.3, bf16[32,128,128]{2,1,0:T(8,128)(2,1)S(1)} %bitcast.54), kind=kLoop, calls=%fused_computation.14 | loop fusion | flops 4718592 | bytes 18874368 | tf_op jit(solution)/shard_map/concatenate | solution.py:27
  144.6 17.6 %gather_fusion.1 = bf16[512,128,128]{2,1,0:T(8,128)(2,1)} fusion(bf16[288,128,128]{2,1,0:T(8,128)(2,1)} %pad_maximum_fusion, s32[1024]{0:T(1024)S(1)} %pad_clamp_fusion), kind=kCustom, calls=%fused_computation.1 | custom fusion | bytes 33556480 | tf_op jit(solution)/shard_map/gather | solution.py:29
  162.3 0.0 copy-start
  162.3 0.0 copy-start.4
  162.3 0.0 copy-start.5
  162.3 13.1 %fusion.4 = f32[32,128,128,1]{2,1,3,0:T(8,128)S(1)} fusion(bf16[32,16,128,128]{3,2,1,0:T(8,128)(2,1)} %bitcast.65, bf16[32,16,128,128]{3,2,1,0:T(8,128)(2,1)} %param.12, bf16[32,16]{1,0:T(8,128)(2,1)S(1)} %fusion.22), kind=kOutput, calls=%fused_computation.12 | convolution fusion | flops 2155872256 | bytes 35652608 | tf_op jit(solution)/shard_map/bsij,bsjr->bir/dot_general | solution.py:28
  175.4 0.0 copy-done
  175.4 0.0 copy-done.4
  175.4 0.0 copy-done.5
  175.4 1.0 fusion.23
  176.4 8.6 %gather_fusion.2 = bf16[256,128,128]{2,1,0:T(8,128)(2,1)} fusion(bf16[32,128,128]{2,1,0:T(8,128)(2,1)S(1)} %bitcast.55, s32[1024]{0:T(1024)S(1)} %pad_clamp_fusion.1), kind=kCustom, calls=%fused_computation.2 | custom fusion | bytes 16778240 | tf_op jit(solution)/shard_map/gather | solution.py:23
  185.1 104.6 %all_to_all.15 = bf16[128,2,128,128]{3,2,1,0:T(8,128)(2,1)} all-to-all(bf16[128,2,128,128]{3,2,1,0:T(8,128)(2,1)} %bitcast.63), channel_id=1, replica_groups=mesh['rows'=32,'cores'=4] {'rows','cores'}, dimensions={0} | all-to-all | bytes 16777216 | tf_op jit(solution)/shard_map/all_to_all | solution.py:24
  289.7 7.8 %pad_maximum_fusion.1 = bf16[288,128,128]{2,1,0:T(8,128)(2,1)} fusion(bf16[256,128,128]{2,1,0:T(8,128)(2,1)} %bitcast.60, bf16[32,128,128]{2,1,0:T(8,128)(2,1)S(1)} %bitcast.56), kind=kLoop, calls=%fused_computation.15 | loop fusion | flops 4718592 | bytes 18874368 | tf_op jit(solution)/shard_map/concatenate | solution.py:27
  297.5 17.6 %gather_fusion.3 = bf16[512,128,128]{2,1,0:T(8,128)(2,1)} fusion(bf16[288,128,128]{2,1,0:T(8,128)(2,1)} %pad_maximum_fusion.1, s32[1024]{0:T(1024)S(1)} %pad_clamp_fusion), kind=kCustom, calls=%fused_computation.3 | custom fusion | bytes 33556480 | tf_op jit(solution)/shard_map/gather | solution.py:29
  315.2 0.0 copy-start.1
  315.2 13.1 %fusion.2 = f32[32,128,128,1]{2,1,3,0:T(8,128)S(1)} fusion(bf16[32,16,128,128]{3,2,1,0:T(8,128)(2,1)} %bitcast.66, bf16[32,16,128,128]{3,2,1,0:T(8,128)(2,1)} %param.12, bf16[32,16]{1,0:T(8,128)(2,1)S(1)} %fusion.22), kind=kOutput, calls=%fused_computation.10 | convolution fusion | flops 2155872256 | bytes 35652608 | tf_op jit(solution)/shard_map/bsij,bsjr->bir/dot_general | solution.py:28
  328.3 0.0 copy-start.7
  328.3 0.0 copy-done.1
  328.3 2.0 fusion.15
  330.3 0.0 copy-done.7
  330.3 0.0 copy-start.6
  330.3 26.4 %scatter_custom_fusion = f32[16384,128]{1,0:T(8,128)} fusion(s32[4096]{0:T(1024)S(1)} %copy-done.7, f32[4096,128]{1,0:T(8,128)} %fusion.15, f32[]{:T(128)} %constant.2.clone.1), kind=kCustom, calls=%fused_computation.21 | custom fusion | flops 524288 | bytes 8389120 | tf_op jit(solution)/shard_map/scatter-add | solution.py:35
  356.7 0.0 all-reduce.2.cloned.1.call-update
  356.7 157.7 %all-reduce.2.cloned.1.call-done = f32[16384,128]{1,0:T(8,128)} async-done(((f32[16384,128]{1,0:T(8,128)}), f32[16384,128]{1,0:T(8,128)}) %all-reduce.2.cloned.1.call-update) | async-done | bytes 8388624 | tf_op jit(solution)/shard_map/psum | solution.py:36
  514.4 0.0 copy-done.6
  514.4 6.9 divide_convert_fusion
  521.3 17.1 %gather_fusion.4 = bf16[4096,128]{1,0:T(8,128)(2,1)} fusion(bf16[16384,128]{1,0:T(8,128)(2,1)} %divide_convert_fusion, s32[4096]{0:T(1024)S(1)} %fusion.21), kind=kCustom, calls=%fused_computation.4 | custom fusion | bytes 2113536 | tf_op jit(solution)/shard_map/gather | solution.py:38
  538.4 1.4 fusion.20
  539.8 8.6 %gather_fusion.5 = bf16[256,128,128]{2,1,0:T(8,128)(2,1)} fusion(bf16[32,128,128]{2,1,0:T(8,128)(2,1)S(1)} %bitcast.57, s32[1024]{0:T(1024)S(1)} %pad_clamp_fusion.1), kind=kCustom, calls=%fused_computation.5 | custom fusion | bytes 16778240 | tf_op jit(solution)/shard_map/gather | solution.py:23
  548.4 104.4 %all_to_all.16 = bf16[128,2,128,128]{3,2,1,0:T(8,128)(2,1)} all-to-all(bf16[128,2,128,128]{3,2,1,0:T(8,128)(2,1)} %bitcast.62), channel_id=1, replica_groups=mesh['rows'=32,'cores'=4] {'rows','cores'}, dimensions={0} | all-to-all | bytes 16777216 | tf_op jit(solution)/shard_map/all_to_all | solution.py:24
  652.8 7.8 %pad_maximum_fusion.2 = bf16[288,128,128]{2,1,0:T(8,128)(2,1)} fusion(bf16[256,128,128]{2,1,0:T(8,128)(2,1)} %bitcast.61, bf16[32,128,128]{2,1,0:T(8,128)(2,1)S(1)} %bitcast.58), kind=kLoop, calls=%fused_computation.16 | loop fusion | flops 4718592 | bytes 18874368 | tf_op jit(solution)/shard_map/concatenate | solution.py:27
  660.7 17.6 %gather_fusion.6 = bf16[512,128,128]{2,1,0:T(8,128)(2,1)} fusion(bf16[288,128,128]{2,1,0:T(8,128)(2,1)} %pad_maximum_fusion.2, s32[1024]{0:T(1024)S(1)} %pad_clamp_fusion), kind=kCustom, calls=%fused_computation.6 | custom fusion | bytes 33556480 | tf_op jit(solution)/shard_map/gather | solution.py:29
  678.3 0.0 copy-start.2
  678.3 0.0 copy-start.3
  678.3 13.1 %fusion = f32[32,128,128,1]{2,1,3,0:T(8,128)S(1)} fusion(bf16[32,16,128,128]{3,2,1,0:T(8,128)(2,1)} %bitcast.64, bf16[32,16,128,128]{3,2,1,0:T(8,128)(2,1)} %param.12, bf16[32,16]{1,0:T(8,128)(2,1)S(1)} %fusion.22), kind=kOutput, calls=%fused_computation.8 | convolution fusion | flops 2155872256 | bytes 35652608 | tf_op jit(solution)/shard_map/bsij,bsjr->bir/dot_general | solution.py:28
  691.4 0.0 copy-done.2
  691.4 0.0 copy-done.3
  691.4 2.0 fusion.14
  (4 shorter events, 0.0 us)
Async XLA Ops:
  17.8 11.9 %copy-start.8 = (s32[32,16]{0,1:T(8,128)S(1)}, s32[32,16]{0,1:T(8,128)}, u32[]{:S(2)}) copy-start(s32[32,16]{0,1:T(8,128)} %param.13) | copy-start | bytes 6148
  17.8 12.1 %copy-start.9 = (s32[32]{0:T(128)S(1)}, s32[32]{0:T(128)}, u32[]{:S(2)}) copy-start(s32[32]{0:T(128)} %param.14) | copy-start | bytes 388
  17.8 119.0 %all-to-all-start = ((bf16[128,2,128,128]{3,2,1,0:T(8,128)(2,1)}), bf16[128,2,128,128]{3,2,1,0:T(8,128)(2,1)}, u32[]{:S(2)}, u32[]{:S(2)}) async-start(bf16[128,2,128,128]{3,2,1,0:T(8,128)(2,1)} %bitcast.59), calls=%async_computation | async-start | bytes 16777216 | tf_op jit(solution)/shard_map/all_to_all | solution.py:24
  29.5 484.9 %all-reduce.2.cloned.1.call-start = ((), (), s32[]{:S(2)}) async-start(), calls=%async_computation.3 | async-start | bytes 16777216 | tf_op jit(solution)/shard_map/psum | solution.py:36
  162.3 13.1 %copy-start = (f32[4096,128]{1,0:T(8,128)S(1)}, f32[4096,128]{1,0:T(8,128)}, u32[]{:S(2)}) copy-start(f32[4096,128]{1,0:T(8,128)} %param.9) | copy-start | bytes 6291460
  162.3 13.1 %copy-start.4 = (f32[4096,128]{1,0:T(8,128)S(1)}, f32[4096,128]{1,0:T(8,128)}, u32[]{:S(2)}) copy-start(f32[4096,128]{1,0:T(8,128)} %param.10) | copy-start | bytes 6291460
  162.3 13.1 %copy-start.5 = (f32[4096]{0:T(1024)S(1)}, f32[4096]{0:T(1024)}, u32[]{:S(2)}) copy-start(f32[4096]{0:T(1024)} %param.11) | copy-start | bytes 49156
  315.2 13.1 %copy-start.1 = (f32[4096,128]{1,0:T(8,128)S(1)}, f32[4096,128]{1,0:T(8,128)}, u32[]{:S(2)}) copy-start(f32[4096,128]{1,0:T(8,128)} %param.9) | copy-start | bytes 6291460
  328.3 2.0 copy-start.7
  330.3 184.1 %copy-start.6 = (f32[16384]{0:T(1024)S(1)}, f32[16384]{0:T(1024)}, u32[]{:S(2)}) copy-start(f32[16384]{0:T(1024)} %param.17) | copy-start | bytes 196612
  678.3 13.1 %copy-start.2 = (f32[4096,128]{1,0:T(8,128)S(1)}, f32[4096,128]{1,0:T(8,128)}, u32[]{:S(2)}) copy-start(f32[4096,128]{1,0:T(8,128)} %param.9) | copy-start | bytes 6291460
  678.3 13.1 %copy-start.3 = (bf16[4096,128]{1,0:T(8,128)(2,1)S(1)}, bf16[4096,128]{1,0:T(8,128)(2,1)}, u32[]{:S(2)}) copy-start(bf16[4096,128]{1,0:T(8,128)(2,1)} %gather_fusion.4) | copy-start | bytes 3145732
Sparse Core Ops, SparseCore 0:
  356.8 157.5 all-reduce.1
where the time goes:
time: 702 us; the launch traced here: 700 us
  waiting for transfers between devices  264 us (38%)
  blocking collectives  209 us (30%)
  local copies, waits for them, and re-layouts  96.3 us (14%)
  other arithmetic  65.7 us (9%)
  matrix products  39.3 us (6%)
  between operations  13.6 us (2%)
  starting transfers between devices  11.9 us (2%)
    all_to_all x2, blocking collectives, apply(): lax.all_to_all(outgoing, ('rows', 'cores'), split_axis=0, concat_axis=0,...  209 us
    psum x1, waiting for transfers between devices, body(): total = lax.psum(local_coarse, ('rows', 'cores'))  158 us
    all_to_all x1, waiting for transfers between devices, apply(): lax.all_to_all(outgoing, ('rows', 'cores'), split_axis=0, concat_axis=0,...  107 us
    gather x3, local copies, waits for them, and re-layouts, apply(): table[columns]  52.8 us
    dot_general x3, matrix products, apply(): jnp.einsum('bsij,bsjr->bir', live_weights, table[columns], preferred_elem...  39.3 us
    scatter-add x1, other arithmetic, body(): local_coarse = jax.ops.segment_sum(residue, aggregates, num_segments=NC)  26.4 us
    gather x3, local copies, waits for them, and re-layouts, apply(): outgoing = blocks[my_lists]  25.9 us
    concatenate x3, other arithmetic, apply(): table = jnp.concatenate([blocks, incoming.reshape(-1, blocksize, width)], 0)  23.5 us
  transfers between devices with their start and end apart: 2, of which 2 were waited for; matrix products, arithmetic and copies ran while one was open for 0% of the time, Pallas kernels for 0%

commit v1 on v0

v1 whole, which is shorter than its diff:
```python
import functools

import jax
import jax.numpy as jnp
from jax import lax
from jax.experimental import pallas as pl
from jax.experimental.pallas import tpu as pltpu
from jax.sharding import PartitionSpec as P

ND = 128
NB = 32
BS = 128
NC = 16384
HALF = NC // 2
TB = NB + 2 * ND
damping = 0.7
MESH = pl.DeviceIdType.MESH
VMEM = pltpu.VMEM
SMEM = pltpu.SMEM
f32 = jnp.float32
bf16 = jnp.bfloat16


def my_place():
    me = lax.axis_index("rows") * 4 + lax.axis_index("cores")
    return me, me // 32, lax.rem(me // 8, 4), lax.rem(me, 4), lax.rem(me // 4, 2)


def place_id(x, y, z, c):
    return ((x * 4 + y) * 2 + c, z)


def peer(k, spot):
    me, x, y, z, c = spot
    m = lax.rem(k * 37, 128)
    px = lax.rem(x + m // 32, 4)
    py = lax.rem(y + lax.rem(m // 8, 4), 4)
    pc = lax.rem(c + lax.rem(m // 4, 2), 2)
    pz = lax.rem(z + lax.rem(m, 4), 4)
    return px, py, pz, pc


def column_of(row):
    return jnp.broadcast_to(row, (BS, BS)).T


def offsum(w_ref, t_ref, col_ref, cnt_ref, b):
    cnt = cnt_ref[b]
    acc = None
    for s in range(0, 16, 2):
        c0 = jnp.where(s < cnt, col_ref[b * 16 + s], TB)
        c1 = jnp.where(s + 1 < cnt, col_ref[b * 16 + s + 1], TB)
        lhs = jnp.concatenate([w_ref[b, s], w_ref[b, s + 1]], axis=1)
        rhs = jnp.concatenate([t_ref[c0], t_ref[c1]], axis=0)
        part = jnp.dot(lhs, rhs, preferred_element_type=f32)
        acc = part if acc is None else acc + part
    return acc


def halo_kernel(
    col_ref, cnt_ref, lst_ref, guess_ref, rhs_ref, deg_ref, agg_ref, w_hbm,
    x1_ref, res_ref, ids_ref,
    w_ref, t1, t2, loc, sbuf, idbuf, wsem, ss, rs, idss, idrs,
):
    spot = my_place()
    me = spot[0]
    wcopy = pltpu.make_async_copy(w_hbm, w_ref, wsem)
    wcopy.start()
    bar = pltpu.get_barrier_semaphore()

    def hello(k, _):
        px, py, pz, pc = peer(k, spot)
        pl.semaphore_signal(bar, inc=1, device_id=place_id(px, py, pz, pc), device_id_type=MESH)
        return 0

    lax.fori_loop(1, ND, hello, 0)

    def cast(b, _):
        v = guess_ref[b].astype(bf16)
        t1[b] = v
        loc[b] = v
        return 0

    lax.fori_loop(0, NB, cast, 0)
    t1[TB] = jnp.zeros((BS, BS), bf16)
    t2[TB] = jnp.zeros((BS, BS), bf16)

    def fill(k):
        px, py, pz, pc = peer(k, spot)
        d = ((px * 4 + py) * 2 + pc) * 4 + pz
        for j in range(2):
            sbuf[k, j] = loc[lst_ref[2 * d + j]]

    def send(k, dst, i):
        px, py, pz, pc = peer(k, spot)
        pltpu.make_async_remote_copy(
            sbuf.at[k], dst.at[pl.ds(NB + 2 * me, 2)], ss.at[i], rs.at[i],
            device_id=place_id(px, py, pz, pc), device_id_type=MESH,
        ).start()

    def fill_ids(k, _):
        px, py, pz, pc = peer(k, spot)
        d = ((px * 4 + py) * 2 + pc) * 4 + pz
        for j in range(2):
            idbuf[k, j] = agg_ref[lst_ref[2 * d + j]]
        return 0

    def send_ids(k, _):
        px, py, pz, pc = peer(k, spot)
        pltpu.make_async_remote_copy(
            idbuf.at[k], ids_ref.at[pl.ds(2 * me, 2)], idss, idrs,
            device_id=place_id(px, py, pz, pc), device_id_type=MESH,
        ).start()
        return 0

    def fill1(k, _):
        fill(k)
        return 0

    lax.fori_loop(1, ND, fill1, 0)
    lax.fori_loop(1, ND, fill_ids, 0)
    for j in range(2):
        own = lst_ref[2 * me + j]
        t1[NB + 2 * me + j] = loc[own]
        ids_ref[2 * me + j] = agg_ref[own]
    pl.semaphore_wait(bar, ND - 1)

    def send1(k, _):
        send(k, t1, 0)
        return 0

    lax.fori_loop(1, ND, send1, 0)
    lax.fori_loop(1, ND, send_ids, 0)
    wcopy.wait()

    def wait_all(i):
        pltpu.make_async_copy(t1.at[pl.ds(0, 254)], t1.at[pl.ds(0, 254)], rs.at[i]).wait()
        pltpu.make_async_copy(t1.at[pl.ds(0, 254)], t1.at[pl.ds(0, 254)], ss.at[i]).wait()

    wait_all(0)

    def first(b, _):
        off = offsum(w_ref, t1, col_ref, cnt_ref, b)
        deg = column_of(deg_ref[b])
        g = guess_ref[b]
        x = g + damping * (rhs_ref[b] - (deg * g - off)) / deg
        x1_ref[b] = x
        v = x.astype(bf16)
        t2[b] = v
        loc[b] = v
        return 0

    lax.fori_loop(0, NB, first, 0)

    def fill2(k, _):
        fill(k)

        @pl.when(k > 2)
        def _():
            send(k - 2, t2, 1)

        return 0

    lax.fori_loop(1, ND, fill2, 0)
    send(ND - 2, t2, 1)
    for j in range(2):
        t2[NB + 2 * me + j] = loc[lst_ref[2 * me + j]]
    send(ND - 1, t2, 1)
    wait_all(1)

    def second(b, _):
        off = offsum(w_ref, t2, col_ref, cnt_ref, b)
        deg = column_of(deg_ref[b])
        res_ref[b] = rhs_ref[b] - (deg * x1_ref[b] - off)
        return 0

    lax.fori_loop(0, NB, second, 0)
    pltpu.make_async_copy(ids_ref.at[pl.ds(0, 254)], ids_ref.at[pl.ds(0, 254)], idrs).wait()
    pltpu.make_async_copy(ids_ref.at[pl.ds(0, 254)], ids_ref.at[pl.ds(0, 254)], idss).wait()


def halo(columns, counts, lists, guess, rhs, degree, agg, weights):
    vm = pl.BlockSpec(memory_space=VMEM)
    sm = pl.BlockSpec(memory_space=SMEM)
    return pl.pallas_call(
        halo_kernel,
        out_shape=(
            jax.ShapeDtypeStruct((NB, BS, BS), f32),
            jax.ShapeDtypeStruct((NB, BS, BS), f32),
            jax.ShapeDtypeStruct((2 * ND, 1, BS), jnp.int32),
        ),
        in_specs=[sm, sm, sm, vm, vm, vm, vm, pl.BlockSpec(memory_space=pl.ANY)],
        out_specs=(vm, vm, vm),
        scratch_shapes=[
            VMEM((NB, 16, BS, BS), bf16),
            VMEM((TB + 1, BS, BS), bf16),
            VMEM((TB + 1, BS, BS), bf16),
            VMEM((NB, BS, BS), bf16),
            VMEM((ND, 2, BS, BS), bf16),
            VMEM((ND, 2, 1, BS), jnp.int32),
            pltpu.SemaphoreType.DMA,
            pltpu.SemaphoreType.DMA((2,)),
            pltpu.SemaphoreType.DMA((2,)),
            pltpu.SemaphoreType.DMA,
            pltpu.SemaphoreType.DMA,
        ],
        compiler_params=pltpu.CompilerParams(
            collective_id=0, has_side_effects=True, vmem_limit_bytes=60 * 2**20
        ),
        name="halo",
    )(columns, counts, lists, guess, rhs, degree, agg, weights)


def scatter_kernel(agg_ref, res_ref, out_ref, b1, b2, b3):
    bufs = (out_ref, b1, b2, b3)
    n = 4096 // 4

    def clear(i, _):
        for buf in bufs:
            for u in range(4):
                buf[pl.ds(i * 32 + u * 8, 8), :] = jnp.zeros((8, BS), f32)
        return 0

    lax.fori_loop(0, NC // 32, clear, 0)

    def add(i, _):
        for u in range(8):
            for q, buf in enumerate(bufs):
                r = q * n + i * 8 + u
                a = agg_ref[r]
                buf[pl.ds(a, 1), :] = buf[pl.ds(a, 1), :] + res_ref[pl.ds(r, 1), :]
        return 0

    lax.fori_loop(0, n // 8, add, 0)

    def total(i, _):
        for u in range(4):
            at = pl.ds(i * 32 + u * 8, 8)
            out_ref[at, :] = (out_ref[at, :] + b1[at, :]) + (b2[at, :] + b3[at, :])
        return 0

    lax.fori_loop(0, NC // 32, total, 0)


def scatter(agg, res):
    vm = pl.BlockSpec(memory_space=VMEM)
    return pl.pallas_call(
        scatter_kernel,
        out_shape=jax.ShapeDtypeStruct((NC, BS), f32),
        in_specs=[pl.BlockSpec(memory_space=SMEM), vm],
        out_specs=vm,
        scratch_shapes=[VMEM((NC, BS), f32)] * 3,
        compiler_params=pltpu.CompilerParams(vmem_limit_bytes=48 * 2**20),
        name="scatter",
    )(agg, res)


UNIT = (48, 48, 32)
BASE = (0, 64 * 48, 128 * 48)


def coarse_kernel(diag_ref, coarse_ref, out_ref, swap, r1, r2, r3, s0, q0, s1, q1, s2, q2, s3, q3, a3s, a3r, a2s, a2r, a1s, a1r, cs, cr):
    me, x, y, z, c = my_place()
    xyz = (x, y, z)
    half = c * HALF
    other = (1 - c) * HALF

    def along(dim, k):
        p = [x, y, z]
        p[dim] = lax.rem(p[dim] + k, 4)
        return place_id(p[0], p[1], p[2], c)

    partner = place_id(x, y, z, 1 - c)
    bar = pltpu.get_barrier_semaphore()
    pl.semaphore_signal(bar, inc=1, device_id=partner, device_id_type=MESH)
    for dim in range(3):
        for k in range(1, 4):
            pl.semaphore_signal(bar, inc=1, device_id=along(dim, k), device_id_type=MESH)
    pl.semaphore_wait(bar, 10)

    def rcopy(src, dst, ssem, rsem, dev):
        return pltpu.make_async_remote_copy(src, dst, ssem, rsem, device_id=dev, device_id_type=MESH)

    def add_into(dst, d0, srcs, rows, step=16):
        def go(i, _):
            v = dst[pl.ds(pl.multiple_of(d0 + i * step, 8), step), :]
            for ref, r0 in srcs:
                v = v + ref[pl.ds(pl.multiple_of(r0 + i * step, 8), step), :]
            dst[pl.ds(pl.multiple_of(d0 + i * step, 8), step), :] = v
            return 0

        lax.fori_loop(0, rows // step, go, 0)

    order = ((0, 1, 2), (1, 2, 0), (2, 0, 1))
    swaps = []
    for k in (1, 2, 3, 0):
        for p in range(3):
            rows = UNIT[p] * 16
            a = lax.rem(xyz[order[p][0]] + k, 4)
            at = BASE[p] + a * rows
            cp = rcopy(
                coarse_ref.at[pl.ds(pl.multiple_of(other + at, 16), rows), :],
                swap.at[pl.ds(pl.multiple_of(at, 16), rows), :],
                s0.at[p, k], q0.at[p, k], partner,
            )
            cp.start()
            swaps.append((k, p, at, rows, cp))
    pend = []
    sent1 = {}
    for k, p, at, rows, cp in swaps:
        cp.wait_recv()
        add_into(swap, at, [(coarse_ref, half + at)], rows)
        if k:
            cp1 = rcopy(
                swap.at[pl.ds(pl.multiple_of(at, 16), rows), :],
                r1.at[k - 1, pl.ds(BASE[p] // 4, rows), :],
                s1.at[p, k - 1], q1.at[p, k - 1], along(order[p][0], k),
            )
            sent1[p, k] = cp1
            pend.append(cp1)
        if len(pend) > 1:
            pend.pop(0).start()
    for cp1 in pend:
        cp1.start()
    cur = []
    for p in range(3):
        rows = UNIT[p] * 16
        at = BASE[p] + xyz[order[p][0]] * rows
        for k in range(1, 4):
            sent1[p, k].wait_recv()
        add_into(swap, at, [(r1.at[k], BASE[p] // 4) for k in range(3)], rows)
        cur.append(at)
    sent2 = {}
    for p in range(3):
        rows = UNIT[p] * 4
        for k in range(1, 4):
            a = lax.rem(xyz[order[p][1]] + k, 4)
            sent2[p, k] = rcopy(
                swap.at[pl.ds(pl.multiple_of(cur[p] + a * rows, 16), rows), :],
                r2.at[k - 1, pl.ds(BASE[p] // 16, rows), :],
                s2.at[p, k - 1], q2.at[p, k - 1], along(order[p][1], k),
            )
            sent2[p, k].start()
    for p in range(3):
        rows = UNIT[p] * 4
        at = cur[p] + xyz[order[p][1]] * rows
        for k in range(1, 4):
            sent2[p, k].wait_recv()
        add_into(swap, at, [(r2.at[k], BASE[p] // 16) for k in range(3)], rows)
        cur[p] = at
    sent3 = {}
    for p in range(3):
        rows = UNIT[p]
        for k in range(1, 4):
            a = lax.rem(xyz[order[p][2]] + k, 4)
            sent3[p, k] = rcopy(
                swap.at[pl.ds(pl.multiple_of(cur[p] + a * rows, 16), rows), :],
                r3.at[k - 1, pl.ds(BASE[p] // 64, rows), :],
                s3.at[p, k - 1], q3.at[p, k - 1], along(order[p][2], k),
            )
            sent3[p, k].start()
    for p in range(3):
        rows = UNIT[p]
        at = cur[p] + xyz[order[p][2]] * rows
        for k in range(1, 4):
            sent3[p, k].wait_recv()
        cur[p] = at
        for i in range(rows // 16):
            v = swap[pl.ds(pl.multiple_of(at + i * 16, 8), 16), :]
            for k in range(3):
                v = v + r3[k, pl.ds(BASE[p] // 64 + i * 16, 16), :]
            div = jnp.concatenate(
                [jnp.full((1, BS), diag_ref[half + at + i * 16 + r], f32) for r in range(16)], axis=0
            )
            out_ref[pl.ds(pl.multiple_of(half + at + i * 16, 16), 16), :] = (v / div).astype(bf16)
    sends = list(sent1.values()) + list(sent2.values()) + list(sent3.values()) + [s[4] for s in swaps]

    def spread(sent, p, dim, at, rows, ssem, rsem):
        for k in range(1, 4):
            ref = out_ref.at[pl.ds(pl.multiple_of(half + at, 16), rows), :]
            cp = rcopy(ref, ref, ssem.at[p, k - 1], rsem.at[p, k - 1], along(dim, k))
            cp.start()
            sent[p, k] = cp
            sends.append(cp)

    g3, g2, g1 = {}, {}, {}
    for p in range(3):
        spread(g3, p, order[p][2], cur[p], UNIT[p], a3s, a3r)
    for p in range(3):
        for k in range(1, 4):
            g3[p, k].wait_recv()
        at = cur[p] - xyz[order[p][2]] * UNIT[p]
        cur[p] = at
        spread(g2, p, order[p][1], at, UNIT[p] * 4, a2s, a2r)
    swapped = []

    def hand_over(p, a, k):
        rows = UNIT[p] * 16
        ref = out_ref.at[pl.ds(pl.multiple_of(half + BASE[p] + a * rows, 16), rows), :]
        cp = rcopy(ref, ref, cs.at[p, k], cr.at[p, k], partner)
        cp.start()
        sends.append(cp)
        swapped.append(cp)

    for p in range(3):
        for k in range(1, 4):
            g2[p, k].wait_recv()
        at = cur[p] - xyz[order[p][1]] * UNIT[p] * 4
        cur[p] = at
        spread(g1, p, order[p][0], at, UNIT[p] * 16, a1s, a1r)
        hand_over(p, xyz[order[p][0]], 0)
    for k in range(1, 4):
        for p in range(3):
            g1[p, k].wait_recv()
            hand_over(p, lax.rem(xyz[order[p][0]] + 4 - k, 4), k)
    for cp in swapped:
        cp.wait_recv()
    for cp in sends:
        cp.wait_send()


def coarse_solve(diag, coarse):
    vm = pl.BlockSpec(memory_space=VMEM)
    dma = pltpu.SemaphoreType.DMA
    return pl.pallas_call(
        coarse_kernel,
        out_shape=jax.ShapeDtypeStruct((NC, BS), bf16),
        in_specs=[pl.BlockSpec(memory_space=SMEM), vm],
        out_specs=vm,
        scratch_shapes=[
            VMEM((HALF, BS), f32),
            VMEM((3, HALF // 4, BS), f32),
            VMEM((3, HALF // 16, BS), f32),
            VMEM((3, HALF // 64, BS), f32),
            dma((3, 4)), dma((3, 4)),
            dma((3, 3)), dma((3, 3)), dma((3, 3)), dma((3, 3)), dma((3, 3)), dma((3, 3)),
            dma((3, 3)), dma((3, 3)), dma((3, 3)), dma((3, 3)), dma((3, 3)), dma((3, 3)),
            dma((3, 4)), dma((3, 4)),
        ],
        compiler_params=pltpu.CompilerParams(
            collective_id=1, has_side_effects=True, vmem_limit_bytes=40 * 2**20
        ),
        name="coarse",
    )(diag, coarse)


def final_kernel(
    col_ref, cnt_ref, agg_ref, ids_ref, corr_ref, x1_ref, res_ref, deg_ref, w_hbm,
    out_ref, w_ref, cf, table, pcl, tile, wsem,
):
    wcopy = pltpu.make_async_copy(w_hbm, w_ref, wsem)
    wcopy.start()

    def widen(i, _):
        for u in range(4):
            at = pl.ds(pl.multiple_of(i * 64 + u * 16, 16), 16)
            cf[at, :] = corr_ref[at, :].astype(f32)
        return 0

    lax.fori_loop(0, NC // 64, widen, 0)
    table[TB] = jnp.zeros((BS, BS), bf16)

    def local(b, _):
        for r in range(BS):
            pcl[b, pl.ds(r, 1), :] = cf[pl.ds(agg_ref[b * BS + r], 1), :]
        table[b] = pcl[b].astype(bf16)
        return 0

    lax.fori_loop(0, NB, local, 0)

    def remote(t, _):
        for r in range(BS):
            tile[pl.ds(r, 1), :] = cf[pl.ds(ids_ref[t * BS + r], 1), :]
        table[NB + t] = tile[...].astype(bf16)
        return 0

    lax.fori_loop(0, 2 * ND, remote, 0)
    wcopy.wait()

    def final(b, _):
        off = offsum(w_ref, table, col_ref, cnt_ref, b)
        deg = column_of(deg_ref[b])
        pc = pcl[b]
        out_ref[b] = (x1_ref[b] + pc) + damping * (res_ref[b] - (deg * pc - off)) / deg
        return 0

    lax.fori_loop(0, NB, final, 0)


def final(columns, counts, agg, ids, corr, x1, res, degree, weights):
    vm = pl.BlockSpec(memory_space=VMEM)
    sm = pl.BlockSpec(memory_space=SMEM)
    return pl.pallas_call(
        final_kernel,
        out_shape=jax.ShapeDtypeStruct((NB, BS, BS), f32),
        in_specs=[sm, sm, sm, sm, vm, vm, vm, vm, pl.BlockSpec(memory_space=pl.ANY)],
        out_specs=vm,
        scratch_shapes=[
            VMEM((NB, 16, BS, BS), bf16),
            VMEM((NC, BS), f32),
            VMEM((TB + 1, BS, BS), bf16),
            VMEM((NB, BS, BS), f32),
            VMEM((BS, BS), f32),
            pltpu.SemaphoreType.DMA,
        ],
        compiler_params=pltpu.CompilerParams(vmem_limit_bytes=60 * 2**20),
        name="final",
    )(columns, counts, agg, ids, corr, x1, res, degree, weights)


def body(rhs, guess, degree, weights, columns, block_counts, send_lists, aggregates, coarse_diag):
    cols = columns.reshape(-1)
    lists = send_lists.reshape(-1)
    deg = degree.reshape(NB, 1, BS)
    x1, res, ids = halo(
        cols, block_counts, lists,
        guess.reshape(NB, BS, BS), rhs.reshape(NB, BS, BS), deg,
        aggregates.reshape(NB, 1, BS), weights,
    )
    coarse = scatter(aggregates, res.reshape(NB * BS, BS))
    corr = coarse_solve(coarse_diag, coarse)
    out = final(cols, block_counts, aggregates, ids.reshape(-1), corr, x1, res, deg, weights)
    return out.reshape(NB * BS, BS)


def solution(mesh):
    both = ("rows", "cores")
    return jax.shard_map(
        body,
        mesh=mesh,
        in_specs=(
            P(both, None),
            P(both, None),
            P(both),
            P(both, None, None, None),
            P(both, None),
            P(both),
            P(both, None, None),
            P(both),
            P(),
        ),
        out_specs=P(both, None),
        check_vma=False,
    )
```

time: 702 us -> 394 us (0.56)
  Pallas kernels: 0 us -> 382 us
  waiting for transfers between devices: 264 us -> 0 us
  blocking collectives: 209 us -> 0 us
  local copies, waits for them, and re-layouts: 96.3 us -> 9.78 us
  other arithmetic: 65.7 us -> 0 us
  matrix products: 39.3 us -> 0 us
  between operations: 13.6 us -> 0.05 us
  starting transfers between devices: 11.9 us -> 0 us
    pallas_call x0 -> x4, Pallas kernels: none -> 382 us  [the longest x1 250 us: halo(): pl.pallas_call(halo_kernel, out_shape=(jax.ShapeDtypeStruct((NB, BS, BS),...]
    all_to_all x2 -> x0, blocking collectives: 209 us -> none  [apply(): lax.all_to_all(outgoing, ('rows', 'cores'), split_axis=0, concat_axis=0,...]
    psum x1 -> x0, waiting for transfers between devices: 158 us -> none  [body(): total = lax.psum(local_coarse, ('rows', 'cores'))]
    all_to_all x1 -> x0, waiting for transfers between devices: 107 us -> none  [apply(): lax.all_to_all(outgoing, ('rows', 'cores'), split_axis=0, concat_axis=0,...]
    gather x7 -> x0, local copies, waits for them, and re-layouts: 95.8 us -> none  [the longest x3 52.8 us: apply(): table[columns]]
    dot_general x3 -> x0, matrix products: 39.3 us -> none  [apply(): jnp.einsum('bsij,bsjr->bir', live_weights, table[columns], preferred_elem...]
    scatter-add x1 -> x0, other arithmetic: 26.4 us -> none  [body(): local_coarse = jax.ops.segment_sum(residue, aggregates, num_segments=NC)]
    concatenate x3 -> x0, other arithmetic: 23.5 us -> none  [apply(): table = jnp.concatenate([blocks, incoming.reshape(-1, blocksize, width)], 0)]
  transfers between devices with their start and end apart: 2 -> 0, of which waited for: 2 -> 0; matrix products, arithmetic and copies ran while one was open for 0% -> 0% of each run, Pallas kernels for 0% -> 0%
where the time goes in v1:
time: 394 us; the launch traced here: 392 us
  Pallas kernels  382 us (97%)
  local copies, waits for them, and re-layouts  9.78 us (2%)
    pallas_call x1, Pallas kernels, halo(): pl.pallas_call(halo_kernel, out_shape=(jax.ShapeDtypeStruct((NB, BS, BS),...  250 us
    pallas_call x1, Pallas kernels, coarse_solve(): pl.pallas_call(coarse_kernel, out_shape=jax.ShapeDtypeStruct((NC, BS), bf...  63.4 us
    pallas_call x1, Pallas kernels, final(): pl.pallas_call(final_kernel, out_shape=jax.ShapeDtypeStruct((NB, BS, BS),...  51.3 us
    pallas_call x1, Pallas kernels, scatter(): pl.pallas_call(scatter_kernel, out_shape=jax.ShapeDtypeStruct((NC, BS), f...  17.4 us
    unnamed x12, local copies, waits for them, and re-layouts  8.45 us

profile of v1, /device:TPU:0, one launch (start us, length us, event | category | flops | bytes accessed | tf_op | source)
XLA Modules:
  0.0 392.2 jit_solution(6089148979859314823)
XLA Ops:
  0.0 0.8 copy.10
  0.8 0.6 reshape.27.col_ref
  1.4 0.8 copy.11
  2.2 0.7 reshape.28.lst_ref
  2.9 0.0 copy-start.3
  2.9 250.3 %halo.1 = (f32[32,128,128]{2,1,0:T(8,128)}, f32[32,128,128]{2,1,0:T(8,128)}, s32[256,1,128]{2,1,0:T(1,128)}) custom-call(s32[512]{0:T(512)} %reshape.27.col_ref, s32[32]{0:T(128)} %cnt_ref.3, s32[256]{0:T(256)} %reshape.28.lst_ref, f32[32,128,128]{2,1,0:T(8,128)} %bitcast.9, f32[32,128,128]{2,1,0:T(8,128)} %bitcast.10, f32[32,1,128]{2,1,0:T(1,128)} %bitcast.12, ...), custom_call_target="tpu_custom_call" | custom-call | tf_op jit(solution)/shard_map/halo/pallas_call | solution.py:185
  253.2 0.0 copy-done.3
  253.2 0.0 copy-start.2
  253.2 1.6 copy-done.2
  254.8 0.0 copy-start.4
  254.8 17.4 %scatter.1.coarse_ref = f32[16384,128]{1,0:T(8,128)} custom-call(s32[4096]{0:T(1024)S(1)} %copy-done.3, f32[4096,128]{1,0:T(8,128)S(1)} %bitcast.7), custom_call_target="tpu_custom_call" | custom-call | tf_op jit(solution)/shard_map/scatter/pallas_call | solution.py:247
  272.2 0.0 copy-done.4
  272.2 0.0 copy-start
  272.2 3.4 copy-done
  275.6 63.4 %coarse.1.corr_ref = bf16[16384,128]{1,0:T(8,128)(2,1)S(1)} custom-call(f32[16384]{0:T(1024)S(1)} %copy-done.4, f32[16384,128]{1,0:T(8,128)S(1)} %copy-done), custom_call_target="tpu_custom_call" | custom-call | tf_op jit(solution)/shard_map/coarse/pallas_call | solution.py:425
  339.0 0.0 copy-start.1
  339.0 1.9 copy-done.1
  340.9 51.3 %final.1 = f32[32,128,128]{2,1,0:T(8,128)} custom-call(s32[512]{0:T(512)} %reshape.27.col_ref, s32[32]{0:T(128)} %cnt_ref.3, s32[4096]{0:T(1024)} %agg_ref.3, s32[32768]{0:T(1024)} %bitcast.11, bf16[16384,128]{1,0:T(8,128)(2,1)} %copy-done.1, f32[32,128,128]{2,1,0:T(8,128)} %get-tuple-element.10.x1_ref, f32[32,128,128]{2,1,0:T(8,128)} %get-tuple-element.9.res_ref, ...), custom_call_target="tpu_custom_call" | custom-call | tf_op jit(solution)/shard_map/final/pallas_call | solution.py:493
Async XLA Ops:
  2.9 250.3 %copy-start.3 = (s32[4096]{0:T(1024)S(1)}, s32[4096]{0:T(1024)}, u32[]{:S(2)}) copy-start(s32[4096]{0:T(1024)} %agg_ref.3) | copy-start | bytes 49156
  253.2 1.6 copy-start.2
  254.8 17.4 %copy-start.4 = (f32[16384]{0:T(1024)S(1)}, f32[16384]{0:T(1024)}, u32[]{:S(2)}) copy-start(f32[16384]{0:T(1024)} %diag_ref.1) | copy-start | bytes 196612
  272.2 3.4 copy-start
  339.0 1.9 copy-start.1

commit v2 on v1

v2 whole, which is shorter than its diff:
```python
import functools

import jax
import jax.numpy as jnp
from jax import lax
from jax.experimental import pallas as pl
from jax.experimental.pallas import tpu as pltpu
from jax.sharding import PartitionSpec as P

ND = 128
NB = 32
BS = 128
NC = 16384
HALF = NC // 2
TB = NB + 2 * ND
HUBS = 8
damping = 0.7
MESH = pl.DeviceIdType.MESH
VMEM = pltpu.VMEM
SMEM = pltpu.SMEM
f32 = jnp.float32
bf16 = jnp.bfloat16


def my_place():
    me = lax.axis_index("rows") * 4 + lax.axis_index("cores")
    return me, me // 32, lax.rem(me // 8, 4), lax.rem(me, 4), lax.rem(me // 4, 2)


def place_id(x, y, z, c):
    return ((x * 4 + y) * 2 + c, z)


def peer(k, spot):
    me, x, y, z, c = spot
    m = lax.rem(k * 37, 128)
    px = lax.rem(x + m // 32, 4)
    py = lax.rem(y + lax.rem(m // 8, 4), 4)
    pc = lax.rem(c + lax.rem(m // 4, 2), 2)
    pz = lax.rem(z + lax.rem(m, 4), 4)
    return px, py, pz, pc


def column_of(row):
    return jnp.broadcast_to(row, (BS, BS)).T


def find_hubs(cnt_ref, hub_ref, rank_ref):
    seen = jnp.int32(0)
    at = [jnp.int32(0)] * HUBS
    for b in range(NB):
        rank_ref[b] = seen
        seen = seen + jnp.where(cnt_ref[b] > 8, 1, 0)
        for k in range(HUBS):
            at[k] = at[k] + jnp.where(seen <= k, 1, 0)
    for k in range(HUBS):
        hub_ref[k] = jnp.minimum(at[k], NB - 1)


def half_row(w_ref, t_ref, col_ref, b, s0):
    acc = None
    for s in range(s0, s0 + 8, 2):
        lhs = jnp.concatenate([w_ref[b, s], w_ref[b, s + 1]], axis=1)
        rhs = jnp.concatenate([t_ref[col_ref[s, b]], t_ref[col_ref[s + 1, b]]], axis=0)
        part = jnp.dot(lhs, rhs, preferred_element_type=f32)
        acc = part if acc is None else acc + part
    return acc


def stencil(w_ref, t_ref, col_ref, cnt_ref, hub_ref, rank_ref, hacc, finish, width=4):
    def hubs(i, _):
        for u in range(width):
            k = i * width + u
            hacc[k] = half_row(w_ref, t_ref, col_ref, hub_ref[k], 8)
        return 0

    lax.fori_loop(0, HUBS // width, hubs, 0)

    def rows(i, _):
        for u in range(width):
            b = i * width + u
            extra = hacc[jnp.minimum(rank_ref[b], HUBS - 1)]
            off = half_row(w_ref, t_ref, col_ref, b, 0)
            off = off + jnp.where(cnt_ref[b] > 8, extra, 0.0)
            finish(b, off)
        return 0

    lax.fori_loop(0, NB // width, rows, 0)


def halo_kernel(
    col_ref, cnt_ref, lst_ref, guess_ref, rhs_ref, deg_ref, agg_ref, w_hbm,
    x1_ref, res_ref, ids_ref,
    w_ref, t1, t2, loc, sbuf, idbuf, hacc, hub_ref, rank_ref, wsem, ss, rs, idss, idrs,
):
    spot = my_place()
    me = spot[0]
    wcopy = pltpu.make_async_copy(w_hbm, w_ref, wsem)
    wcopy.start()
    bar = pltpu.get_barrier_semaphore()

    def cast(b, _):
        v = guess_ref[b].astype(bf16)
        t1[b] = v
        loc[b] = v
        return 0

    lax.fori_loop(0, NB, cast, 0)

    def prepare(k, _):
        px, py, pz, pc = peer(k, spot)
        row = (px * 4 + py) * 2 + pc
        d = row * 4 + pz
        pl.semaphore_signal(bar, inc=1, device_id=(row, pz), device_id_type=MESH)
        for j in range(2):
            own = lst_ref[j, d]
            sbuf[k, j] = loc[own]
            idbuf[k, j] = agg_ref[own]
        return 0

    lax.fori_loop(1, ND, prepare, 0)
    for j in range(2):
        own = lst_ref[j, me]
        t1[NB + 2 * me + j] = loc[own]
        ids_ref[2 * me + j] = agg_ref[own]
    pl.semaphore_wait(bar, ND - 1)

    def send(k, dst, i, dev):
        pltpu.make_async_remote_copy(
            sbuf.at[k], dst.at[pl.ds(NB + 2 * me, 2)], ss.at[i], rs.at[i],
            device_id=dev, device_id_type=MESH,
        ).start()

    def send1(k, _):
        px, py, pz, pc = peer(k, spot)
        dev = place_id(px, py, pz, pc)
        pltpu.make_async_remote_copy(
            idbuf.at[k], ids_ref.at[pl.ds(2 * me, 2)], idss, idrs,
            device_id=dev, device_id_type=MESH,
        ).start()
        send(k, t1, 0, dev)
        return 0

    lax.fori_loop(1, ND, send1, 0)
    find_hubs(cnt_ref, hub_ref, rank_ref)
    wcopy.wait()

    def wait_all(i):
        pltpu.make_async_copy(t1.at[pl.ds(0, 254)], t1.at[pl.ds(0, 254)], rs.at[i]).wait()
        pltpu.make_async_copy(t1.at[pl.ds(0, 254)], t1.at[pl.ds(0, 254)], ss.at[i]).wait()

    wait_all(0)

    def first(b, off):
        deg = column_of(deg_ref[b])
        g = guess_ref[b]
        x = g + damping * (rhs_ref[b] - (deg * g - off)) / deg
        x1_ref[b] = x
        v = x.astype(bf16)
        t2[b] = v
        loc[b] = v

    stencil(w_ref, t1, col_ref, cnt_ref, hub_ref, rank_ref, hacc, first)

    def fill2(k, _):
        px, py, pz, pc = peer(k, spot)
        d = ((px * 4 + py) * 2 + pc) * 4 + pz
        for j in range(2):
            sbuf[k, j] = loc[lst_ref[j, d]]

        @pl.when(k > 2)
        def _():
            send(k - 2, t2, 1, place_id(*peer(k - 2, spot)))

        return 0

    lax.fori_loop(1, ND, fill2, 0)
    send(ND - 2, t2, 1, place_id(*peer(ND - 2, spot)))
    for j in range(2):
        t2[NB + 2 * me + j] = loc[lst_ref[j, me]]
    send(ND - 1, t2, 1, place_id(*peer(ND - 1, spot)))
    wait_all(1)

    def second(b, off):
        deg = column_of(deg_ref[b])
        res_ref[b] = rhs_ref[b] - (deg * x1_ref[b] - off)

    stencil(w_ref, t2, col_ref, cnt_ref, hub_ref, rank_ref, hacc, second)
    pltpu.make_async_copy(ids_ref.at[pl.ds(0, 254)], ids_ref.at[pl.ds(0, 254)], idrs).wait()
    pltpu.make_async_copy(ids_ref.at[pl.ds(0, 254)], ids_ref.at[pl.ds(0, 254)], idss).wait()


def halo(columns, counts, lists, guess, rhs, degree, agg, weights):
    vm = pl.BlockSpec(memory_space=VMEM)
    sm = pl.BlockSpec(memory_space=SMEM)
    return pl.pallas_call(
        halo_kernel,
        out_shape=(
            jax.ShapeDtypeStruct((NB, BS, BS), f32),
            jax.ShapeDtypeStruct((NB, BS, BS), f32),
            jax.ShapeDtypeStruct((2 * ND, 1, BS), jnp.int32),
        ),
        in_specs=[sm, sm, sm, vm, vm, vm, vm, pl.BlockSpec(memory_space=pl.ANY)],
        out_specs=(vm, vm, vm),
        scratch_shapes=[
            VMEM((NB, 16, BS, BS), bf16),
            VMEM((TB, BS, BS), bf16),
            VMEM((TB, BS, BS), bf16),
            VMEM((NB, BS, BS), bf16),
            VMEM((ND, 2, BS, BS), bf16),
            VMEM((ND, 2, 1, BS), jnp.int32),
            VMEM((HUBS, BS, BS), f32),
            SMEM((HUBS,), jnp.int32),
            SMEM((NB,), jnp.int32),
            pltpu.SemaphoreType.DMA,
            pltpu.SemaphoreType.DMA((2,)),
            pltpu.SemaphoreType.DMA((2,)),
            pltpu.SemaphoreType.DMA,
            pltpu.SemaphoreType.DMA,
        ],
        compiler_params=pltpu.CompilerParams(
            collective_id=0, has_side_effects=True, vmem_limit_bytes=60 * 2**20
        ),
        name="halo",
    )(columns, counts, lists, guess, rhs, degree, agg, weights)


def scatter_kernel(agg_ref, res_hbm, out_hbm, b0, b1, b2, b3, res_ref, rsem, osem):
    bufs = (b0, b1, b2, b3)
    n = 4096 // 4
    rcopy = pltpu.make_async_copy(res_hbm, res_ref, rsem)
    rcopy.start()

    def clear(i, _):
        for buf in bufs:
            for u in range(8):
                buf[pl.ds(i * 64 + u * 8, 8), :] = jnp.zeros((8, BS), f32)
        return 0

    lax.fori_loop(0, NC // 64, clear, 0)
    rcopy.wait()

    def add(i, _):
        for u in range(8):
            for q, buf in enumerate(bufs):
                r = q * n + i * 8 + u
                a = agg_ref[r]
                buf[pl.ds(a, 1), :] = buf[pl.ds(a, 1), :] + res_ref[pl.ds(r, 1), :]
        return 0

    lax.fori_loop(0, n // 8, add, 0)
    chunk = NC // 8
    outs = []
    for c in range(8):

        def total(i, _):
            for u in range(8):
                at = pl.ds(c * chunk + i * 64 + u * 8, 8)
                b0[at, :] = (b0[at, :] + b1[at, :]) + (b2[at, :] + b3[at, :])
            return 0

        lax.fori_loop(0, chunk // 64, total, 0)
        part = pl.ds(c * chunk, chunk)
        cp = pltpu.make_async_copy(b0.at[part, :], out_hbm.at[part, :], osem.at[c])
        outs.append(cp)
        if c:
            outs[c - 1].start()
    outs[-1].start()
    for cp in outs:
        cp.wait()


def scatter(agg, res):
    hbm = pl.BlockSpec(memory_space=pltpu.HBM)
    return pl.pallas_call(
        scatter_kernel,
        out_shape=jax.ShapeDtypeStruct((NC, BS), f32),
        in_specs=[pl.BlockSpec(memory_space=SMEM), hbm],
        out_specs=hbm,
        scratch_shapes=[VMEM((NC, BS), f32)] * 4
        + [VMEM((NB * BS, BS), f32), pltpu.SemaphoreType.DMA, pltpu.SemaphoreType.DMA((8,))],
        compiler_params=pltpu.CompilerParams(vmem_limit_bytes=63 * 2**20),
        name="scatter",
    )(agg, res)


UNIT = (48, 48, 32)
BASE = (0, 64 * 48, 128 * 48)


def coarse_kernel(
    col_ref, cnt_ref, diag_ref, deg_ref, agg_hbm, ids_hbm, coarse_hbm, x1_hbm, res_hbm, w_hbm,
    out_ref,
    w_ref, x1_ref, res_ref, agg_ref, ids_ref, acc, swap, r1, r2, r3, corr, cf, table, pcl, tile0, tile1,
    hacc, hub_ref, rank_ref, lsem, hsem, s0, q0, s1, q1, s2, q2, s3, q3,
    a3s, a3r, a2s, a2r, a1s, a1r, cs, cr,
):
    me, x, y, z, c = my_place()
    xyz = (x, y, z)
    half = c * HALF
    other = (1 - c) * HALF

    def along(dim, k):
        p = [x, y, z]
        p[dim] = lax.rem(p[dim] + k, 4)
        return place_id(p[0], p[1], p[2], c)

    partner = place_id(x, y, z, 1 - c)
    bar = pltpu.get_barrier_semaphore()
    pl.semaphore_signal(bar, inc=1, device_id=partner, device_id_type=MESH)
    for dim in range(3):
        for k in range(1, 4):
            pl.semaphore_signal(bar, inc=1, device_id=along(dim, k), device_id_type=MESH)

    def rcopy(src, dst, ssem, rsem, dev):
        return pltpu.make_async_remote_copy(src, dst, ssem, rsem, device_id=dev, device_id_type=MESH)

    def rows_at(at, rows):
        return pl.ds(pl.multiple_of(at, 16), rows)

    def add_into(dst, d0, srcs, rows, step=32):
        if rows % step:
            step = 16

        def go(i, _):
            v = dst[rows_at(d0 + i * step, step), :]
            for ref, r0 in srcs:
                v = v + ref[rows_at(r0 + i * step, step), :]
            dst[rows_at(d0 + i * step, step), :] = v
            return 0

        lax.fori_loop(0, rows // step, go, 0)

    order = ((0, 1, 2), (1, 2, 0), (2, 0, 1))
    pieces = []
    for k in (1, 2, 3, 0):
        for p in range(3):
            rows = UNIT[p] * 16
            at = BASE[p] + lax.rem(xyz[order[p][0]] + k, 4) * rows
            hcopy = pltpu.make_async_copy(
                coarse_hbm.at[rows_at(half + at, rows), :], acc.at[rows_at(at, rows), :], hsem.at[p, k]
            )
            hcopy.start()
            pieces.append((k, p, at, rows, hcopy))
    pl.semaphore_wait(bar, 10)
    sends = []
    swaps = []
    for k, p, at, rows, hcopy in pieces:
        cp = rcopy(
            coarse_hbm.at[rows_at(other + at, rows), :], swap.at[rows_at(at, rows), :],
            s0.at[p, k], q0.at[p, k], partner,
        )
        cp.start()
        swaps.append(cp)
    loads = [
        pltpu.make_async_copy(src, dst, lsem.at[i])
        for i, (src, dst) in enumerate(
            ((w_hbm, w_ref), (x1_hbm, x1_ref), (res_hbm, res_ref), (agg_hbm, agg_ref), (ids_hbm, ids_ref))
        )
    ]
    pend = []
    sent1 = {}
    for (k, p, at, rows, hcopy), cp in zip(pieces, swaps):
        hcopy.wait()
        cp.wait_recv()
        add_into(acc, at, [(swap, at)], rows)
        if k:
            cp1 = rcopy(
                acc.at[rows_at(at, rows), :], r1.at[k - 1, pl.ds(BASE[p] // 4, rows), :],
                s1.at[p, k - 1], q1.at[p, k - 1], along(order[p][0], k),
            )
            sent1[p, k] = cp1
            pend.append(cp1)
        if len(pend) > 1:
            pend.pop(0).start()
    for cp1 in pend:
        cp1.start()
    for cp in loads:
        cp.start()
    find_hubs(cnt_ref, hub_ref, rank_ref)
    cur = []
    sent2 = {}
    for p in (2, 0, 1):
        rows = UNIT[p] * 16
        at = BASE[p] + xyz[order[p][0]] * rows
        for k in range(1, 4):
            sent1[p, k].wait_recv()
        add_into(acc, at, [(r1.at[k], BASE[p] // 4) for k in range(3)], rows)
        n2 = UNIT[p] * 4
        for k in range(1, 4):
            a = lax.rem(xyz[order[p][1]] + k, 4)
            sent2[p, k] = rcopy(
                acc.at[rows_at(at + a * n2, n2), :], r2.at[k - 1, pl.ds(BASE[p] // 16, n2), :],
                s2.at[p, k - 1], q2.at[p, k - 1], along(order[p][1], k),
            )
            sent2[p, k].start()
        cur.append((p, at + xyz[order[p][1]] * n2))
    sent3 = {}
    last = []
    for p, at in cur:
        rows = UNIT[p] * 4
        for k in range(1, 4):
            sent2[p, k].wait_recv()
        add_into(acc, at, [(r2.at[k], BASE[p] // 16) for k in range(3)], rows)
        n3 = UNIT[p]
        for k in range(1, 4):
            a = lax.rem(xyz[order[p][2]] + k, 4)
            sent3[p, k] = rcopy(
                acc.at[rows_at(at + a * n3, n3), :], r3.at[k - 1, pl.ds(BASE[p] // 64, n3), :],
                s3.at[p, k - 1], q3.at[p, k - 1], along(order[p][2], k),
            )
            sent3[p, k].start()
        last.append((p, at + xyz[order[p][2]] * n3))

    def spread(sent, p, dim, at, rows, ssem, rsem):
        for k in range(1, 4):
            ref = corr.at[rows_at(half + at, rows), :]
            cp = rcopy(ref, ref, ssem.at[p, k - 1], rsem.at[p, k - 1], along(dim, k))
            cp.start()
            sent[p, k] = cp
            sends.append(cp)

    def widen(at, rows):
        def go(i, _):
            here = rows_at(at + i * 16, 16)
            cf[here, :] = corr[here, :].astype(f32)
            return 0

        lax.fori_loop(0, rows // 16, go, 0)

    g3, g2, g1 = {}, {}, {}
    for p, at in last:
        rows = UNIT[p]
        for k in range(1, 4):
            sent3[p, k].wait_recv()
        for i in range(rows // 16):
            v = acc[rows_at(at + i * 16, 16), :]
            for k in range(3):
                v = v + r3[k, pl.ds(BASE[p] // 64 + i * 16, 16), :]
            div = jnp.concatenate(
                [jnp.full((1, BS), diag_ref[half + at + i * 16 + r], f32) for r in range(16)], axis=0
            )
            corr[rows_at(half + at + i * 16, 16), :] = (v / div).astype(bf16)
        spread(g3, p, order[p][2], at, rows, a3s, a3r)
    cur = []
    for p, at in last:
        for k in range(1, 4):
            g3[p, k].wait_recv()
        at = at - xyz[order[p][2]] * UNIT[p]
        cur.append((p, at))
        spread(g2, p, order[p][1], at, UNIT[p] * 4, a2s, a2r)
    swapped = []

    def hand_over(p, a, k):
        rows = UNIT[p] * 16
        ref = corr.at[rows_at(half + BASE[p] + a * rows, rows), :]
        cp = rcopy(ref, ref, cs.at[p, k], cr.at[p, k], partner)
        cp.start()
        sends.append(cp)
        swapped.append((cp, other + BASE[p] + a * rows, rows))
        widen(half + BASE[p] + a * rows, rows)

    for p, at in cur:
        for k in range(1, 4):
            g2[p, k].wait_recv()
        at = at - xyz[order[p][1]] * UNIT[p] * 4
        spread(g1, p, order[p][0], at, UNIT[p] * 16, a1s, a1r)
        hand_over(p, xyz[order[p][0]], 0)
    for k in (1, 3, 2):
        for p in (2, 0, 1):
            g1[p, k].wait_recv()
            hand_over(p, lax.rem(xyz[order[p][0]] + 4 - k, 4), k)
    for cp, at, rows in swapped:
        cp.wait_recv()
        widen(at, rows)
    for cp in loads:
        cp.wait()

    def local(b, _):
        for r in range(BS):
            pcl[b, pl.ds(r, 1), :] = cf[pl.ds(agg_ref[b * BS + r], 1), :]

        @pl.when(b > 0)
        def _():
            table[b - 1] = pcl[b - 1].astype(bf16)

        return 0

    lax.fori_loop(0, NB, local, 0)
    table[NB - 1] = pcl[NB - 1].astype(bf16)

    def pick(t, tile):
        for r in range(BS):
            tile[pl.ds(r, 1), :] = cf[pl.ds(ids_ref[t * BS + r], 1), :]

    pick(0, tile0)

    def remote(i, _):
        t = 2 * i
        pick(t + 1, tile1)
        table[NB + t] = tile0[...].astype(bf16)
        pick(t + 2, tile0)
        table[NB + t + 1] = tile1[...].astype(bf16)
        return 0

    lax.fori_loop(0, ND - 1, remote, 0)
    pick(2 * ND - 1, tile1)
    table[TB - 2] = tile0[...].astype(bf16)
    table[TB - 1] = tile1[...].astype(bf16)

    def third(b, off):
        deg = column_of(deg_ref[b])
        pc = pcl[b]
        out_ref[b] = (x1_ref[b] + pc) + damping * (res_ref[b] - (deg * pc - off)) / deg

    stencil(w_ref, table, col_ref, cnt_ref, hub_ref, rank_ref, hacc, third)
    for cp in list(sent1.values()) + list(sent2.values()) + list(sent3.values()) + swaps + sends:
        cp.wait_send()


def coarse_leg(columns, counts, diag, degree, agg, ids, coarse, x1, res, weights):
    vm = pl.BlockSpec(memory_space=VMEM)
    sm = pl.BlockSpec(memory_space=SMEM)
    hbm = pl.BlockSpec(memory_space=pltpu.HBM)
    dma = pltpu.SemaphoreType.DMA
    return pl.pallas_call(
        coarse_kernel,
        out_shape=jax.ShapeDtypeStruct((NB, BS, BS), f32),
        in_specs=[sm, sm, sm, vm, hbm, hbm, hbm, hbm, hbm, hbm],
        out_specs=vm,
        scratch_shapes=[
            VMEM((NB, 16, BS, BS), bf16),
            VMEM((NB, BS, BS), f32),
            VMEM((NB, BS, BS), f32),
            SMEM((NB * BS,), jnp.int32),
            SMEM((2 * ND * BS,), jnp.int32),
            VMEM((HALF, BS), f32),
            VMEM((HALF, BS), f32),
            VMEM((3, HALF // 4, BS), f32),
            VMEM((3, HALF // 16, BS), f32),
            VMEM((3, HALF // 64, BS), f32),
            VMEM((NC, BS), bf16),
            VMEM((NC, BS), f32),
            VMEM((TB, BS, BS), bf16),
            VMEM((NB, BS, BS), f32),
            VMEM((BS, BS), f32),
            VMEM((BS, BS), f32),
            VMEM((HUBS, BS, BS), f32),
            SMEM((HUBS,), jnp.int32),
            SMEM((NB,), jnp.int32),
            dma((5,)),
            dma((3, 4)), dma((3, 4)), dma((3, 4)),
            dma((3, 3)), dma((3, 3)), dma((3, 3)), dma((3, 3)), dma((3, 3)), dma((3, 3)),
            dma((3, 3)), dma((3, 3)), dma((3, 3)), dma((3, 3)), dma((3, 3)), dma((3, 3)),
            dma((3, 4)), dma((3, 4)),
        ],
        compiler_params=pltpu.CompilerParams(
            collective_id=1, has_side_effects=True, vmem_limit_bytes=63 * 2**20
        ),
        name="coarse_leg",
    )(columns, counts, diag, degree, agg, ids, coarse, x1, res, weights)


def body(rhs, guess, degree, weights, columns, block_counts, send_lists, aggregates, coarse_diag):
    cols = columns.T
    lists = send_lists[0].T
    deg = degree.reshape(NB, 1, BS)
    x1, res, ids = halo(
        cols, block_counts, lists,
        guess.reshape(NB, BS, BS), rhs.reshape(NB, BS, BS), deg,
        aggregates.reshape(NB, 1, BS), weights,
    )
    coarse = scatter(aggregates, res.reshape(NB * BS, BS))
    out = coarse_leg(
        cols, block_counts, coarse_diag, deg, aggregates, ids.reshape(-1), coarse, x1, res, weights
    )
    return out.reshape(NB * BS, BS)


def solution(mesh):
    both = ("rows", "cores")
    return jax.shard_map(
        body,
        mesh=mesh,
        in_specs=(
            P(both, None),
            P(both, None),
            P(both),
            P(both, None, None, None),
            P(both, None),
            P(both),
            P(both, None, None),
            P(both),
            P(),
        ),
        out_specs=P(both, None),
        check_vma=False,
    )
```

time: 394 us -> 366 us (0.929)
  Pallas kernels: 382 us -> 362 us
  local copies, waits for them, and re-layouts: 9.78 us -> 3.05 us
    pallas_call x2 -> x1, Pallas kernels: 115 us -> 106 us  [coarse_leg(): pl.pallas_call(coarse_kernel, out_shape=jax.ShapeDtypeStruct((NB, BS, BS)...]
    pallas_call x1, Pallas kernels: 250 us -> 243 us  [halo(): pl.pallas_call(halo_kernel, out_shape=(jax.ShapeDtypeStruct((NB, BS, BS),...]
    unnamed x12 -> x1, local copies, waits for them, and re-layouts: 8.45 us -> 3.05 us
    pallas_call x1, Pallas kernels: 17.4 us -> 13.2 us  [scatter(): pl.pallas_call(scatter_kernel, out_shape=jax.ShapeDtypeStruct((NC, BS), f...]
where the time goes in v2:
time: 366 us
  Pallas kernels  362 us (99%)
    pallas_call x1, Pallas kernels, halo(): pl.pallas_call(halo_kernel, out_shape=(jax.ShapeDtypeStruct((NB, BS, BS),...  243 us
    pallas_call x1, Pallas kernels, coarse_leg(): pl.pallas_call(coarse_kernel, out_shape=jax.ShapeDtypeStruct((NB, BS, BS)...  106 us
    pallas_call x1, Pallas kernels, scatter(): pl.pallas_call(scatter_kernel, out_shape=jax.ShapeDtypeStruct((NC, BS), f...  13.2 us

profile of v2, /device:TPU:0, one launch (start us, length us, event | category | flops | bytes accessed | tf_op | source)
XLA Modules:
  0.0 365.5 jit_solution(14365657110466521662)
XLA Ops:
  0.0 243.0 %halo.1 = (f32[32,128,128]{2,1,0:T(8,128)}, f32[32,128,128]{2,1,0:T(8,128)}, s32[256,1,128]{2,1,0:T(1,128)}) custom-call(s32[16,32]{1,0:T(8,128)} %bitcast.19, s32[32]{0:T(128)} %cnt_ref.3, s32[2,128]{1,0:T(2,128)} %bitcast.21, f32[32,128,128]{2,1,0:T(8,128)} %bitcast.13, f32[32,128,128]{2,1,0:T(8,128)} %bitcast.14, f32[32,1,128]{2,1,0:T(1,128)} %bitcast.17, ...), custom_call_target="tpu_custom_call" | custom-call | tf_op jit(solution)/shard_map/halo/pallas_call | solution.py:196
  243.0 13.2 %scatter.1.coarse_hbm = f32[16384,128]{1,0:T(8,128)} custom-call(s32[4096]{0:T(1024)} %agg_hbm.1, f32[4096,128]{1,0:T(8,128)} %bitcast.11), custom_call_target="tpu_custom_call" | custom-call | tf_op jit(solution)/shard_map/scatter/pallas_call | solution.py:275
  256.3 106.2 %coarse_leg.1 = f32[32,128,128]{2,1,0:T(8,128)} custom-call(s32[16,32]{1,0:T(8,128)} %bitcast.20, s32[32]{0:T(128)} %cnt_ref.3, f32[16384]{0:T(1024)} %diag_ref.1, f32[32,1,128]{2,1,0:T(1,128)} %bitcast.18, s32[4096]{0:T(1024)} %agg_hbm.1, s32[32768]{0:T(1024)} %bitcast.16, f32[16384,128]{1,0:T(8,128)} %scatter.1.coarse_hbm, ...), custom_call_target="tpu_custom_call" | custom-call | tf_op jit(solution)/shard_map/coarse_leg/pallas_call | solution.py:526
  362.5 3.0 copy.11

commit v3 on v2

--- a/solution.py
+++ b/solution.py
@@ -13,6 +13,7 @@
 NC = 16384
 HALF = NC // 2
 TB = NB + 2 * ND
+GROUP = 8
 HUBS = 8
 damping = 0.7
 MESH = pl.DeviceIdType.MESH
@@ -33,7 +34,7 @@
 
 def peer(k, spot):
     me, x, y, z, c = spot
-    m = lax.rem(k * 37, 128)
+    m = lax.rem(k * 19, 128)
     px = lax.rem(x + m // 32, 4)
     py = lax.rem(y + lax.rem(m // 8, 4), 4)
     pc = lax.rem(c + lax.rem(m // 4, 2), 2)
@@ -99,6 +100,13 @@
     wcopy.start()
     bar = pltpu.get_barrier_semaphore()
 
+    def hello(k, _):
+        d = lax.rem(me + k, ND)
+        pl.semaphore_signal(bar, inc=1, device_id=(d // 4, lax.rem(d, 4)), device_id_type=MESH)
+        return 0
+
+    lax.fori_loop(1, ND, hello, 0)
+
     def cast(b, _):
         v = guess_ref[b].astype(bf16)
         t1[b] = v
@@ -111,7 +119,6 @@
         px, py, pz, pc = peer(k, spot)
         row = (px * 4 + py) * 2 + pc
         d = row * 4 + pz
-        pl.semaphore_signal(bar, inc=1, device_id=(row, pz), device_id_type=MESH)
         for j in range(2):
             own = lst_ref[j, d]
             sbuf[k, j] = loc[own]
@@ -291,8 +298,8 @@
 def coarse_kernel(
     col_ref, cnt_ref, diag_ref, deg_ref, agg_hbm, ids_hbm, coarse_hbm, x1_hbm, res_hbm, w_hbm,
     out_ref,
-    w_ref, x1_ref, res_ref, agg_ref, ids_ref, acc, swap, r1, r2, r3, corr, cf, table, pcl, tile0, tile1,
-    hacc, hub_ref, rank_ref, lsem, hsem, s0, q0, s1, q1, s2, q2, s3, q3,
+    w_ref, x1_ref, res_ref, id0, id1, id2, id3, acc, swap, sb1, r1, r2, r3, corr, cf, table, pcl, tile0, tile1,
+    hacc, hub_ref, rank_ref, lsem, isem, hsem, s0, q0, s1, q1, s2, q2, s3, q3,
     a3s, a3r, a2s, a2r, a1s, a1r, cs, cr,
 ):
     me, x, y, z, c = my_place()
@@ -325,11 +332,19 @@
         def go(i, _):
             v = dst[rows_at(d0 + i * step, step), :]
             for ref, r0 in srcs:
-                v = v + ref[rows_at(r0 + i * step, step), :]
+                v = v + ref[rows_at(r0 + i * step, step), :].astype(f32)
             dst[rows_at(d0 + i * step, step), :] = v
             return 0
 
         lax.fori_loop(0, rows // step, go, 0)
+
+    def pack_sum(dst, d0, at, rows):
+        def go(i, _):
+            here = rows_at(at + i * 16, 16)
+            dst[rows_at(d0 + i * 16, 16), :] = (acc[here, :] + swap[here, :]).astype(bf16)
+            return 0
+
+        lax.fori_loop(0, rows // 16, go, 0)
 
     order = ((0, 1, 2), (1, 2, 0), (2, 0, 1))
     pieces = []
@@ -355,7 +370,7 @@
     loads = [
         pltpu.make_async_copy(src, dst, lsem.at[i])
         for i, (src, dst) in enumerate(
-            ((w_hbm, w_ref), (x1_hbm, x1_ref), (res_hbm, res_ref), (agg_hbm, agg_ref), (ids_hbm, ids_ref))
+            ((w_hbm, w_ref), (x1_hbm, x1_ref), (res_hbm, res_ref))
         )
     ]
     pend = []
@@ -363,10 +378,12 @@
     for (k, p, at, rows, hcopy), cp in zip(pieces, swaps):
         hcopy.wait()
         cp.wait_recv()
-        add_into(acc, at, [(swap, at)], rows)
-        if k:
+        if k == 0:
+            add_into(acc, at, [(swap, at)], rows)
+        else:
+            pack_sum(sb1.at[k - 1], BASE[p] // 4, at, rows)
             cp1 = rcopy(
-                acc.at[rows_at(at, rows), :], r1.at[k - 1, pl.ds(BASE[p] // 4, rows), :],
+                sb1.at[k - 1, pl.ds(BASE[p] // 4, rows), :], r1.at[k - 1, pl.ds(BASE[p] // 4, rows), :],
                 s1.at[p, k - 1], q1.at[p, k - 1], along(order[p][0], k),
             )
             sent1[p, k] = cp1
@@ -378,6 +395,15 @@
     for cp in loads:
         cp.start()
     find_hubs(cnt_ref, hub_ref, rank_ref)
+    id_refs = (id0, id1, id2, id3)
+
+    def fetch(src, n, g):
+        part = src.at[pl.ds(pl.multiple_of(n * GROUP * BS, GROUP * BS), GROUP * BS)]
+        return pltpu.make_async_copy(part, id_refs[g], isem.at[g])
+
+    for g in range(2):
+        fetch(agg_hbm, g, g).start()
+        fetch(ids_hbm, g + 2, g + 2).start()
     cur = []
     sent2 = {}
     for p in (2, 0, 1):
@@ -476,37 +502,49 @@
     for cp in loads:
         cp.wait()
 
-    def local(b, _):
-        for r in range(BS):
-            pcl[b, pl.ds(r, 1), :] = cf[pl.ds(agg_ref[b * BS + r], 1), :]
-
-        @pl.when(b > 0)
-        def _():
-            table[b - 1] = pcl[b - 1].astype(bf16)
-
-        return 0
-
-    lax.fori_loop(0, NB, local, 0)
-    table[NB - 1] = pcl[NB - 1].astype(bf16)
-
-    def pick(t, tile):
-        for r in range(BS):
-            tile[pl.ds(r, 1), :] = cf[pl.ds(ids_ref[t * BS + r], 1), :]
-
-    pick(0, tile0)
+    def local(i, _):
+        for g in range(2):
+            n = 2 * i + g
+            fetch(agg_hbm, n, g).wait()
+            for u in range(GROUP):
+                b = n * GROUP + u
+                for r in range(BS):
+                    pcl[b, pl.ds(r, 1), :] = cf[pl.ds(id_refs[g][u * BS + r], 1), :]
+                if u:
+                    table[b - 1] = pcl[b - 1].astype(bf16)
+            table[b] = pcl[b].astype(bf16)
+
+            @pl.when(i == 0)
+            def _():
+                fetch(agg_hbm, n + 2, g).start()
+
+        return 0
+
+    lax.fori_loop(0, 2, local, 0)
+    for g in range(2):
+        fetch(ids_hbm, g, g).start()
+    tiles = (tile0, tile1)
 
     def remote(i, _):
-        t = 2 * i
-        pick(t + 1, tile1)
-        table[NB + t] = tile0[...].astype(bf16)
-        pick(t + 2, tile0)
-        table[NB + t + 1] = tile1[...].astype(bf16)
-        return 0
-
-    lax.fori_loop(0, ND - 1, remote, 0)
-    pick(2 * ND - 1, tile1)
-    table[TB - 2] = tile0[...].astype(bf16)
-    table[TB - 1] = tile1[...].astype(bf16)
+        for g in range(4):
+            n = 4 * i + g
+            fetch(ids_hbm, n, g).wait()
+            for u in range(GROUP):
+                t = NB + n * GROUP + u
+                tile = tiles[u % 2]
+                for r in range(BS):
+                    tile[pl.ds(r, 1), :] = cf[pl.ds(id_refs[g][u * BS + r], 1), :]
+                if u:
+                    table[t - 1] = tiles[(u - 1) % 2][...].astype(bf16)
+            table[t] = tile[...].astype(bf16)
+
+            @pl.when(i < 2 * ND // GROUP // 4 - 1)
+            def _():
+                fetch(ids_hbm, n + 4, g).start()
+
+        return 0
+
+    lax.fori_loop(0, 2 * ND // GROUP // 4, remote, 0)
 
     def third(b, off):
         deg = column_of(deg_ref[b])
@@ -532,11 +570,14 @@
             VMEM((NB, 16, BS, BS), bf16),
             VMEM((NB, BS, BS), f32),
             VMEM((NB, BS, BS), f32),
-            SMEM((NB * BS,), jnp.int32),
-            SMEM((2 * ND * BS,), jnp.int32),
+            SMEM((GROUP * BS,), jnp.int32),
+            SMEM((GROUP * BS,), jnp.int32),
+            SMEM((GROUP * BS,), jnp.int32),
+            SMEM((GROUP * BS,), jnp.int32),
             VMEM((HALF, BS), f32),
             VMEM((HALF, BS), f32),
-            VMEM((3, HALF // 4, BS), f32),
+            VMEM((3, HALF // 4, BS), bf16),
+            VMEM((3, HALF // 4, BS), bf16),
             VMEM((3, HALF // 16, BS), f32),
             VMEM((3, HALF // 64, BS), f32),
             VMEM((NC, BS), bf16),
@@ -548,7 +589,7 @@
             VMEM((HUBS, BS, BS), f32),
             SMEM((HUBS,), jnp.int32),
             SMEM((NB,), jnp.int32),
-            dma((5,)),
+            dma((3,)), dma((4,)),
             dma((3, 4)), dma((3, 4)), dma((3, 4)),
             dma((3, 3)), dma((3, 3)), dma((3, 3)), dma((3, 3)), dma((3, 3)), dma((3, 3)),
             dma((3, 3)), dma((3, 3)), dma((3, 3)), dma((3, 3)), dma((3, 3)), dma((3, 3)),

time: 366 us -> 326 us (0.89)
  Pallas kernels: 362 us -> 323 us
    pallas_call x1, Pallas kernels: 243 us -> 223 us  [halo(): pl.pallas_call(halo_kernel, out_shape=(jax.ShapeDtypeStruct((NB, BS, BS),...]
    pallas_call x1, Pallas kernels: 106 us -> 86.6 us  [coarse_leg(): pl.pallas_call(coarse_kernel, out_shape=jax.ShapeDtypeStruct((NB, BS, BS)...]
where the time goes in v3:
time: 326 us
  Pallas kernels  323 us (99%)
    pallas_call x1, Pallas kernels, halo(): pl.pallas_call(halo_kernel, out_shape=(jax.ShapeDtypeStruct((NB, BS, BS),...  223 us
    pallas_call x1, Pallas kernels, coarse_leg(): pl.pallas_call(coarse_kernel, out_shape=jax.ShapeDtypeStruct((NB, BS, BS)...  86.6 us
    pallas_call x1, Pallas kernels, scatter(): pl.pallas_call(scatter_kernel, out_shape=jax.ShapeDtypeStruct((NC, BS), f...  13.2 us

profile of v3, /device:TPU:0, one launch (start us, length us, event | category | flops | bytes accessed | tf_op | source)
XLA Modules:
  0.0 326.0 jit_solution(2540625042436361640)
XLA Ops:
  0.0 223.2 %halo.1 = (f32[32,128,128]{2,1,0:T(8,128)}, f32[32,128,128]{2,1,0:T(8,128)}, s32[256,1,128]{2,1,0:T(1,128)}) custom-call(s32[16,32]{1,0:T(8,128)} %bitcast.19, s32[32]{0:T(128)} %cnt_ref.3, s32[2,128]{1,0:T(2,128)} %bitcast.21, f32[32,128,128]{2,1,0:T(8,128)} %bitcast.13, f32[32,128,128]{2,1,0:T(8,128)} %bitcast.14, f32[32,1,128]{2,1,0:T(1,128)} %bitcast.17, ...), custom_call_target="tpu_custom_call" | custom-call | tf_op jit(solution)/shard_map/halo/pallas_call | solution.py:203
  223.2 13.2 %scatter.1.coarse_hbm = f32[16384,128]{1,0:T(8,128)} custom-call(s32[4096]{0:T(1024)} %agg_hbm.1, f32[4096,128]{1,0:T(8,128)} %bitcast.11), custom_call_target="tpu_custom_call" | custom-call | tf_op jit(solution)/shard_map/scatter/pallas_call | solution.py:282
  236.4 86.6 %coarse_leg.1 = f32[32,128,128]{2,1,0:T(8,128)} custom-call(s32[16,32]{1,0:T(8,128)} %bitcast.20, s32[32]{0:T(128)} %cnt_ref.3, f32[16384]{0:T(1024)} %diag_ref.1, f32[32,1,128]{2,1,0:T(1,128)} %bitcast.18, s32[4096]{0:T(1024)} %agg_hbm.1, s32[32768]{0:T(1024)} %bitcast.16, f32[16384,128]{1,0:T(8,128)} %scatter.1.coarse_hbm, ...), custom_call_target="tpu_custom_call" | custom-call | tf_op jit(solution)/shard_map/coarse_leg/pallas_call | solution.py:564
  323.0 3.0 copy.11

commit v4 on v3

--- a/solution.py
+++ b/solution.py
@@ -90,14 +90,12 @@
 
 
 def halo_kernel(
-    col_ref, cnt_ref, lst_ref, guess_ref, rhs_ref, deg_ref, agg_ref, w_hbm,
+    col_ref, cnt_ref, lst_ref, guess_hbm, rhs_hbm, deg_ref, agg_ref, w_hbm,
     x1_ref, res_ref, ids_ref,
-    w_ref, t1, t2, loc, sbuf, idbuf, hacc, hub_ref, rank_ref, wsem, ss, rs, idss, idrs,
+    w_ref, guess_ref, rhs_ref, t1, t2, loc, sbuf, idbuf, hacc, hub_ref, rank_ref, lsem, ss, rs, idss, idrs,
 ):
     spot = my_place()
     me = spot[0]
-    wcopy = pltpu.make_async_copy(w_hbm, w_ref, wsem)
-    wcopy.start()
     bar = pltpu.get_barrier_semaphore()
 
     def hello(k, _):
@@ -105,7 +103,14 @@
         pl.semaphore_signal(bar, inc=1, device_id=(d // 4, lax.rem(d, 4)), device_id_type=MESH)
         return 0
 
+    gcopy = pltpu.make_async_copy(guess_hbm, guess_ref, lsem.at[0])
+    gcopy.start()
     lax.fori_loop(1, ND, hello, 0)
+    gcopy.wait()
+    loads = [
+        pltpu.make_async_copy(rhs_hbm, rhs_ref, lsem.at[1]),
+        pltpu.make_async_copy(w_hbm, w_ref, lsem.at[2]),
+    ]
 
     def cast(b, _):
         v = guess_ref[b].astype(bf16)
@@ -114,43 +119,62 @@
         return 0
 
     lax.fori_loop(0, NB, cast, 0)
-
-    def prepare(k, _):
+    pl.semaphore_wait(bar, ND - 1)
+
+    def send(k, dst, i):
+        pltpu.make_async_remote_copy(
+            sbuf.at[k], dst.at[pl.ds(NB + 2 * me, 2)], ss.at[i], rs.at[i],
+            device_id=place_id(*peer(k, spot)), device_id_type=MESH,
+        ).start()
+
+    def send_field(dst, i):
+        def fill(k, _):
+            px, py, pz, pc = peer(k, spot)
+            d = ((px * 4 + py) * 2 + pc) * 4 + pz
+            for j in range(2):
+                sbuf[k, j] = loc[lst_ref[j, d]]
+
+            @pl.when(k > 2)
+            def _():
+                send(k - 2, dst, i)
+
+            return 0
+
+        lax.fori_loop(1, ND, fill, 0)
+        send(ND - 2, dst, i)
+        for j in range(2):
+            dst[NB + 2 * me + j] = loc[lst_ref[j, me]]
+        send(ND - 1, dst, i)
+
+    send_field(t1, 0)
+    for cp in loads:
+        cp.start()
+
+    def send_ids(k, _):
         px, py, pz, pc = peer(k, spot)
         row = (px * 4 + py) * 2 + pc
-        d = row * 4 + pz
         for j in range(2):
-            own = lst_ref[j, d]
-            sbuf[k, j] = loc[own]
-            idbuf[k, j] = agg_ref[own]
-        return 0
-
-    lax.fori_loop(1, ND, prepare, 0)
-    for j in range(2):
-        own = lst_ref[j, me]
-        t1[NB + 2 * me + j] = loc[own]
-        ids_ref[2 * me + j] = agg_ref[own]
-    pl.semaphore_wait(bar, ND - 1)
-
-    def send(k, dst, i, dev):
-        pltpu.make_async_remote_copy(
-            sbuf.at[k], dst.at[pl.ds(NB + 2 * me, 2)], ss.at[i], rs.at[i],
-            device_id=dev, device_id_type=MESH,
-        ).start()
-
-    def send1(k, _):
-        px, py, pz, pc = peer(k, spot)
-        dev = place_id(px, py, pz, pc)
+            idbuf[k, j] = agg_ref[lst_ref[j, row * 4 + pz]]
+
+        @pl.when(k > 1)
+        def _():
+            ship_ids(k - 1)
+
+        return 0
+
+    def ship_ids(k):
         pltpu.make_async_remote_copy(
             idbuf.at[k], ids_ref.at[pl.ds(2 * me, 2)], idss, idrs,
-            device_id=dev, device_id_type=MESH,
+            device_id=place_id(*peer(k, spot)), device_id_type=MESH,
         ).start()
-        send(k, t1, 0, dev)
-        return 0
-
-    lax.fori_loop(1, ND, send1, 0)
+
+    lax.fori_loop(1, ND, send_ids, 0)
+    for j in range(2):
+        ids_ref[2 * me + j] = agg_ref[lst_ref[j, me]]
+    ship_ids(ND - 1)
     find_hubs(cnt_ref, hub_ref, rank_ref)
-    wcopy.wait()
+    for cp in loads:
+        cp.wait()
 
     def wait_all(i):
         pltpu.make_async_copy(t1.at[pl.ds(0, 254)], t1.at[pl.ds(0, 254)], rs.at[i]).wait()
@@ -169,23 +193,7 @@
 
     stencil(w_ref, t1, col_ref, cnt_ref, hub_ref, rank_ref, hacc, first)
 
-    def fill2(k, _):
-        px, py, pz, pc = peer(k, spot)
-        d = ((px * 4 + py) * 2 + pc) * 4 + pz
-        for j in range(2):
-            sbuf[k, j] = loc[lst_ref[j, d]]
-
-        @pl.when(k > 2)
-        def _():
-            send(k - 2, t2, 1, place_id(*peer(k - 2, spot)))
-
-        return 0
-
-    lax.fori_loop(1, ND, fill2, 0)
-    send(ND - 2, t2, 1, place_id(*peer(ND - 2, spot)))
-    for j in range(2):
-        t2[NB + 2 * me + j] = loc[lst_ref[j, me]]
-    send(ND - 1, t2, 1, place_id(*peer(ND - 1, spot)))
+    send_field(t2, 1)
     wait_all(1)
 
     def second(b, off):
@@ -198,6 +206,7 @@
 
 
 def halo(columns, counts, lists, guess, rhs, degree, agg, weights):
+    hbm = pl.BlockSpec(memory_space=pltpu.HBM)
     vm = pl.BlockSpec(memory_space=VMEM)
     sm = pl.BlockSpec(memory_space=SMEM)
     return pl.pallas_call(
@@ -207,10 +216,12 @@
             jax.ShapeDtypeStruct((NB, BS, BS), f32),
             jax.ShapeDtypeStruct((2 * ND, 1, BS), jnp.int32),
         ),
-        in_specs=[sm, sm, sm, vm, vm, vm, vm, pl.BlockSpec(memory_space=pl.ANY)],
+        in_specs=[sm, sm, sm, hbm, hbm, vm, vm, hbm],
         out_specs=(vm, vm, vm),
         scratch_shapes=[
             VMEM((NB, 16, BS, BS), bf16),
+            VMEM((NB, BS, BS), f32),
+            VMEM((NB, BS, BS), f32),
             VMEM((TB, BS, BS), bf16),
             VMEM((TB, BS, BS), bf16),
             VMEM((NB, BS, BS), bf16),
@@ -219,7 +230,7 @@
             VMEM((HUBS, BS, BS), f32),
             SMEM((HUBS,), jnp.int32),
             SMEM((NB,), jnp.int32),
-            pltpu.SemaphoreType.DMA,
+            pltpu.SemaphoreType.DMA((3,)),
             pltpu.SemaphoreType.DMA((2,)),
             pltpu.SemaphoreType.DMA((2,)),
             pltpu.SemaphoreType.DMA,
@@ -291,14 +302,16 @@
     )(agg, res)
 
 
-UNIT = (48, 48, 32)
-BASE = (0, 64 * 48, 128 * 48)
+UNIT = (32, 32, 16, 16, 16, 16)
+PARTS = len(UNIT)
+PACE = (2, 0, 1, 3, 4, 5)
+BASE = tuple(64 * sum(UNIT[:p]) for p in range(PARTS))
 
 
 def coarse_kernel(
     col_ref, cnt_ref, diag_ref, deg_ref, agg_hbm, ids_hbm, coarse_hbm, x1_hbm, res_hbm, w_hbm,
     out_ref,
-    w_ref, x1_ref, res_ref, id0, id1, id2, id3, acc, swap, sb1, r1, r2, r3, corr, cf, table, pcl, tile0, tile1,
+    w_ref, x1_ref, res_ref, id0, id1, id2, id3, acc, swap, r1, r2, r3, corr, cf, table, pcl, tile0, tile1,
     hacc, hub_ref, rank_ref, lsem, isem, hsem, s0, q0, s1, q1, s2, q2, s3, q3,
     a3s, a3r, a2s, a2r, a1s, a1r, cs, cr,
 ):
@@ -332,31 +345,22 @@
         def go(i, _):
             v = dst[rows_at(d0 + i * step, step), :]
             for ref, r0 in srcs:
-                v = v + ref[rows_at(r0 + i * step, step), :].astype(f32)
+                v = v + ref[rows_at(r0 + i * step, step), :]
             dst[rows_at(d0 + i * step, step), :] = v
             return 0
 
         lax.fori_loop(0, rows // step, go, 0)
 
-    def pack_sum(dst, d0, at, rows):
-        def go(i, _):
-            here = rows_at(at + i * 16, 16)
-            dst[rows_at(d0 + i * 16, 16), :] = (acc[here, :] + swap[here, :]).astype(bf16)
-            return 0
-
-        lax.fori_loop(0, rows // 16, go, 0)
-
-    order = ((0, 1, 2), (1, 2, 0), (2, 0, 1))
+    order = ((0, 1, 2), (1, 2, 0), (2, 0, 1)) * (PARTS // 3)
     pieces = []
-    for k in (1, 2, 3, 0):
-        for p in range(3):
-            rows = UNIT[p] * 16
-            at = BASE[p] + lax.rem(xyz[order[p][0]] + k, 4) * rows
-            hcopy = pltpu.make_async_copy(
-                coarse_hbm.at[rows_at(half + at, rows), :], acc.at[rows_at(at, rows), :], hsem.at[p, k]
-            )
-            hcopy.start()
-            pieces.append((k, p, at, rows, hcopy))
+    for k, p in [(k, p + g) for g in range(0, PARTS, 3) for k in (1, 3, 2, 0) for p in range(3)]:
+        rows = UNIT[p] * 16
+        at = BASE[p] + lax.rem(xyz[order[p][0]] + k, 4) * rows
+        hcopy = pltpu.make_async_copy(
+            coarse_hbm.at[rows_at(half + at, rows), :], acc.at[rows_at(at, rows), :], hsem.at[p, k]
+        )
+        hcopy.start()
+        pieces.append((k, p, at, rows, hcopy))
     pl.semaphore_wait(bar, 10)
     sends = []
     swaps = []
@@ -378,12 +382,10 @@
     for (k, p, at, rows, hcopy), cp in zip(pieces, swaps):
         hcopy.wait()
         cp.wait_recv()
-        if k == 0:
-            add_into(acc, at, [(swap, at)], rows)
-        else:
-            pack_sum(sb1.at[k - 1], BASE[p] // 4, at, rows)
+        add_into(acc, at, [(swap, at)], rows)
+        if k:
             cp1 = rcopy(
-                sb1.at[k - 1, pl.ds(BASE[p] // 4, rows), :], r1.at[k - 1, pl.ds(BASE[p] // 4, rows), :],
+                acc.at[rows_at(at, rows), :], r1.at[k - 1, pl.ds(BASE[p] // 4, rows), :],
                 s1.at[p, k - 1], q1.at[p, k - 1], along(order[p][0], k),
             )
             sent1[p, k] = cp1
@@ -406,7 +408,7 @@
         fetch(ids_hbm, g + 2, g + 2).start()
     cur = []
     sent2 = {}
-    for p in (2, 0, 1):
+    for p in PACE:
         rows = UNIT[p] * 16
         at = BASE[p] + xyz[order[p][0]] * rows
         for k in range(1, 4):
@@ -492,10 +494,9 @@
         at = at - xyz[order[p][1]] * UNIT[p] * 4
         spread(g1, p, order[p][0], at, UNIT[p] * 16, a1s, a1r)
         hand_over(p, xyz[order[p][0]], 0)
-    for k in (1, 3, 2):
-        for p in (2, 0, 1):
-            g1[p, k].wait_recv()
-            hand_over(p, lax.rem(xyz[order[p][0]] + 4 - k, 4), k)
+    for k, p in [(k, p) for g in range(0, PARTS, 3) for k in (1, 3, 2) for p in PACE[g : g + 3]]:
+        g1[p, k].wait_recv()
+        hand_over(p, lax.rem(xyz[order[p][0]] + 4 - k, 4), k)
     for cp, at, rows in swapped:
         cp.wait_recv()
         widen(at, rows)
@@ -576,8 +577,7 @@
             SMEM((GROUP * BS,), jnp.int32),
             VMEM((HALF, BS), f32),
             VMEM((HALF, BS), f32),
-            VMEM((3, HALF // 4, BS), bf16),
-            VMEM((3, HALF // 4, BS), bf16),
+            VMEM((3, HALF // 4, BS), f32),
             VMEM((3, HALF // 16, BS), f32),
             VMEM((3, HALF // 64, BS), f32),
             VMEM((NC, BS), bf16),
@@ -590,10 +590,10 @@
             SMEM((HUBS,), jnp.int32),
             SMEM((NB,), jnp.int32),
             dma((3,)), dma((4,)),
-            dma((3, 4)), dma((3, 4)), dma((3, 4)),
-            dma((3, 3)), dma((3, 3)), dma((3, 3)), dma((3, 3)), dma((3, 3)), dma((3, 3)),
-            dma((3, 3)), dma((3, 3)), dma((3, 3)), dma((3, 3)), dma((3, 3)), dma((3, 3)),
-            dma((3, 4)), dma((3, 4)),
+            dma((PARTS, 4)), dma((PARTS, 4)), dma((PARTS, 4)),
+            dma((PARTS, 3)), dma((PARTS, 3)), dma((PARTS, 3)), dma((PARTS, 3)), dma((PARTS, 3)), dma((PARTS, 3)),
+            dma((PARTS, 3)), dma((PARTS, 3)), dma((PARTS, 3)), dma((PARTS, 3)), dma((PARTS, 3)), dma((PARTS, 3)),
+            dma((PARTS, 4)), dma((PARTS, 4)),
         ],
         compiler_params=pltpu.CompilerParams(
             collective_id=1, has_side_effects=True, vmem_limit_bytes=63 * 2**20

time: 326 us -> 338 us (1.037)
  Pallas kernels: 323 us -> 335 us
    pallas_call x1, Pallas kernels: 223 us -> 233 us  [halo(): pl.pallas_call(halo_kernel, out_shape=(jax.ShapeDtypeStruct((NB, BS, BS),...]
where the time goes in v4:
time: 338 us
  Pallas kernels  335 us (99%)
    pallas_call x1, Pallas kernels, halo(): pl.pallas_call(halo_kernel, out_shape=(jax.ShapeDtypeStruct((NB, BS, BS),...  233 us
    pallas_call x1, Pallas kernels, coarse_leg(): pl.pallas_call(coarse_kernel, out_shape=jax.ShapeDtypeStruct((NB, BS, BS)...  88.5 us
    pallas_call x1, Pallas kernels, scatter(): pl.pallas_call(scatter_kernel, out_shape=jax.ShapeDtypeStruct((NC, BS), f...  13.2 us

profile of v4, /device:TPU:0, one launch (start us, length us, event | category | flops | bytes accessed | tf_op | source)
XLA Modules:
  0.0 337.9 jit_solution(11565838291592767775)
XLA Ops:
  0.0 233.1 %halo.1 = (f32[32,128,128]{2,1,0:T(8,128)}, f32[32,128,128]{2,1,0:T(8,128)}, s32[256,1,128]{2,1,0:T(1,128)}) custom-call(s32[16,32]{1,0:T(8,128)} %bitcast.19, s32[32]{0:T(128)} %cnt_ref.3, s32[2,128]{1,0:T(2,128)} %bitcast.21, f32[32,128,128]{2,1,0:T(8,128)} %bitcast.13, f32[32,128,128]{2,1,0:T(8,128)} %bitcast.14, f32[32,1,128]{2,1,0:T(1,128)} %bitcast.17, ...), custom_call_target="tpu_custom_call" | custom-call | tf_op jit(solution)/shard_map/halo/pallas_call | solution.py:212
  233.1 13.2 %scatter.1.coarse_hbm = f32[16384,128]{1,0:T(8,128)} custom-call(s32[4096]{0:T(1024)} %agg_hbm.1, f32[4096,128]{1,0:T(8,128)} %bitcast.11), custom_call_target="tpu_custom_call" | custom-call | tf_op jit(solution)/shard_map/scatter/pallas_call | solution.py:293
  246.3 88.5 %coarse_leg.1 = f32[32,128,128]{2,1,0:T(8,128)} custom-call(s32[16,32]{1,0:T(8,128)} %bitcast.20, s32[32]{0:T(128)} %cnt_ref.3, f32[16384]{0:T(1024)} %diag_ref.1, f32[32,1,128]{2,1,0:T(1,128)} %bitcast.18, s32[4096]{0:T(1024)} %agg_hbm.1, s32[32768]{0:T(1024)} %bitcast.16, f32[16384,128]{1,0:T(8,128)} %scatter.1.coarse_hbm, ...), custom_call_target="tpu_custom_call" | custom-call | tf_op jit(solution)/shard_map/coarse_leg/pallas_call | solution.py:565
  334.9 3.0 copy.11

commit v5 on v3

--- a/solution.py
+++ b/solution.py
@@ -291,14 +291,16 @@
     )(agg, res)
 
 
-UNIT = (48, 48, 32)
-BASE = (0, 64 * 48, 128 * 48)
+UNIT = (32, 32, 16, 16, 16, 16)
+PARTS = len(UNIT)
+PACE = (2, 0, 1, 3, 4, 5)
+BASE = tuple(64 * sum(UNIT[:p]) for p in range(PARTS))
 
 
 def coarse_kernel(
     col_ref, cnt_ref, diag_ref, deg_ref, agg_hbm, ids_hbm, coarse_hbm, x1_hbm, res_hbm, w_hbm,
     out_ref,
-    w_ref, x1_ref, res_ref, id0, id1, id2, id3, acc, swap, sb1, r1, r2, r3, corr, cf, table, pcl, tile0, tile1,
+    w_ref, x1_ref, res_ref, id0, id1, id2, id3, acc, swap, r1, r2, r3, corr, cf, table, pcl, tile0, tile1,
     hacc, hub_ref, rank_ref, lsem, isem, hsem, s0, q0, s1, q1, s2, q2, s3, q3,
     a3s, a3r, a2s, a2r, a1s, a1r, cs, cr,
 ):
@@ -332,31 +334,22 @@
         def go(i, _):
             v = dst[rows_at(d0 + i * step, step), :]
             for ref, r0 in srcs:
-                v = v + ref[rows_at(r0 + i * step, step), :].astype(f32)
+                v = v + ref[rows_at(r0 + i * step, step), :]
             dst[rows_at(d0 + i * step, step), :] = v
             return 0
 
         lax.fori_loop(0, rows // step, go, 0)
 
-    def pack_sum(dst, d0, at, rows):
-        def go(i, _):
-            here = rows_at(at + i * 16, 16)
-            dst[rows_at(d0 + i * 16, 16), :] = (acc[here, :] + swap[here, :]).astype(bf16)
-            return 0
-
-        lax.fori_loop(0, rows // 16, go, 0)
-
-    order = ((0, 1, 2), (1, 2, 0), (2, 0, 1))
+    order = ((0, 1, 2), (1, 2, 0), (2, 0, 1)) * (PARTS // 3)
     pieces = []
-    for k in (1, 2, 3, 0):
-        for p in range(3):
-            rows = UNIT[p] * 16
-            at = BASE[p] + lax.rem(xyz[order[p][0]] + k, 4) * rows
-            hcopy = pltpu.make_async_copy(
-                coarse_hbm.at[rows_at(half + at, rows), :], acc.at[rows_at(at, rows), :], hsem.at[p, k]
-            )
-            hcopy.start()
-            pieces.append((k, p, at, rows, hcopy))
+    for k, p in [(k, p + g) for g in range(0, PARTS, 3) for k in (1, 3, 2, 0) for p in range(3)]:
+        rows = UNIT[p] * 16
+        at = BASE[p] + lax.rem(xyz[order[p][0]] + k, 4) * rows
+        hcopy = pltpu.make_async_copy(
+            coarse_hbm.at[rows_at(half + at, rows), :], acc.at[rows_at(at, rows), :], hsem.at[p, k]
+        )
+        hcopy.start()
+        pieces.append((k, p, at, rows, hcopy))
     pl.semaphore_wait(bar, 10)
     sends = []
     swaps = []
@@ -378,12 +371,10 @@
     for (k, p, at, rows, hcopy), cp in zip(pieces, swaps):
         hcopy.wait()
         cp.wait_recv()
-        if k == 0:
-            add_into(acc, at, [(swap, at)], rows)
-        else:
-            pack_sum(sb1.at[k - 1], BASE[p] // 4, at, rows)
+        add_into(acc, at, [(swap, at)], rows)
+        if k:
             cp1 = rcopy(
-                sb1.at[k - 1, pl.ds(BASE[p] // 4, rows), :], r1.at[k - 1, pl.ds(BASE[p] // 4, rows), :],
+                acc.at[rows_at(at, rows), :], r1.at[k - 1, pl.ds(BASE[p] // 4, rows), :],
                 s1.at[p, k - 1], q1.at[p, k - 1], along(order[p][0], k),
             )
             sent1[p, k] = cp1
@@ -406,7 +397,7 @@
         fetch(ids_hbm, g + 2, g + 2).start()
     cur = []
     sent2 = {}
-    for p in (2, 0, 1):
+    for p in PACE:
         rows = UNIT[p] * 16
         at = BASE[p] + xyz[order[p][0]] * rows
         for k in range(1, 4):
@@ -492,10 +483,9 @@
         at = at - xyz[order[p][1]] * UNIT[p] * 4
         spread(g1, p, order[p][0], at, UNIT[p] * 16, a1s, a1r)
         hand_over(p, xyz[order[p][0]], 0)
-    for k in (1, 3, 2):
-        for p in (2, 0, 1):
-            g1[p, k].wait_recv()
-            hand_over(p, lax.rem(xyz[order[p][0]] + 4 - k, 4), k)
+    for k, p in [(k, p) for g in range(0, PARTS, 3) for k in (1, 3, 2) for p in PACE[g : g + 3]]:
+        g1[p, k].wait_recv()
+        hand_over(p, lax.rem(xyz[order[p][0]] + 4 - k, 4), k)
     for cp, at, rows in swapped:
         cp.wait_recv()
         widen(at, rows)
@@ -563,7 +553,7 @@
     dma = pltpu.SemaphoreType.DMA
     return pl.pallas_call(
         coarse_kernel,
-        out_shape=jax.ShapeDtypeStruct((NB, BS, BS), f32),
+        out_shape=VMEM((NB, BS, BS), f32),
         in_specs=[sm, sm, sm, vm, hbm, hbm, hbm, hbm, hbm, hbm],
         out_specs=vm,
         scratch_shapes=[
@@ -576,8 +566,7 @@
             SMEM((GROUP * BS,), jnp.int32),
             VMEM((HALF, BS), f32),
             VMEM((HALF, BS), f32),
-            VMEM((3, HALF // 4, BS), bf16),
-            VMEM((3, HALF // 4, BS), bf16),
+            VMEM((3, HALF // 4, BS), f32),
             VMEM((3, HALF // 16, BS), f32),
             VMEM((3, HALF // 64, BS), f32),
             VMEM((NC, BS), bf16),
@@ -590,13 +579,13 @@
             SMEM((HUBS,), jnp.int32),
             SMEM((NB,), jnp.int32),
             dma((3,)), dma((4,)),
-            dma((3, 4)), dma((3, 4)), dma((3, 4)),
-            dma((3, 3)), dma((3, 3)), dma((3, 3)), dma((3, 3)), dma((3, 3)), dma((3, 3)),
-            dma((3, 3)), dma((3, 3)), dma((3, 3)), dma((3, 3)), dma((3, 3)), dma((3, 3)),
-            dma((3, 4)), dma((3, 4)),
+            dma((PARTS, 4)), dma((PARTS, 4)), dma((PARTS, 4)),
+            dma((PARTS, 3)), dma((PARTS, 3)), dma((PARTS, 3)), dma((PARTS, 3)), dma((PARTS, 3)), dma((PARTS, 3)),
+            dma((PARTS, 3)), dma((PARTS, 3)), dma((PARTS, 3)), dma((PARTS, 3)), dma((PARTS, 3)), dma((PARTS, 3)),
+            dma((PARTS, 4)), dma((PARTS, 4)),
         ],
         compiler_params=pltpu.CompilerParams(
-            collective_id=1, has_side_effects=True, vmem_limit_bytes=63 * 2**20
+            collective_id=1, has_side_effects=True, vmem_limit_bytes=60 * 2**20
         ),
         name="coarse_leg",
     )(columns, counts, diag, degree, agg, ids, coarse, x1, res, weights)

time: 326 us -> 330 us (1.012)
  Pallas kernels: 323 us -> 328 us
    pallas_call x1, Pallas kernels: 86.6 us -> 91.6 us  [coarse_leg(): pl.pallas_call(coarse_kernel, out_shape=VMEM((NB, BS, BS), f32), in_specs...]
where the time goes in v5:
time: 330 us; the launch traced here: 329 us
  Pallas kernels  328 us (99%)
    pallas_call x1, Pallas kernels, halo(): pl.pallas_call(halo_kernel, out_shape=(jax.ShapeDtypeStruct((NB, BS, BS),...  223 us
    pallas_call x1, Pallas kernels, coarse_leg(): pl.pallas_call(coarse_kernel, out_shape=VMEM((NB, BS, BS), f32), in_specs...  91.6 us
    pallas_call x1, Pallas kernels, scatter(): pl.pallas_call(scatter_kernel, out_shape=jax.ShapeDtypeStruct((NC, BS), f...  13.2 us

profile of v5, /device:TPU:0, one launch (start us, length us, event | category | flops | bytes accessed | tf_op | source)
XLA Modules:
  0.0 329.3 jit_solution(11486279338043783725)
XLA Ops:
  0.0 223.2 %halo.1 = (f32[32,128,128]{2,1,0:T(8,128)}, f32[32,128,128]{2,1,0:T(8,128)}, s32[256,1,128]{2,1,0:T(1,128)}) custom-call(s32[16,32]{1,0:T(8,128)} %bitcast.19, s32[32]{0:T(128)} %cnt_ref.3, s32[2,128]{1,0:T(2,128)} %bitcast.21, f32[32,128,128]{2,1,0:T(8,128)} %bitcast.13, f32[32,128,128]{2,1,0:T(8,128)} %bitcast.14, f32[32,1,128]{2,1,0:T(1,128)} %bitcast.17, ...), custom_call_target="tpu_custom_call" | custom-call | tf_op jit(solution)/shard_map/halo/pallas_call | solution.py:203
  223.2 13.2 %scatter.1.coarse_hbm = f32[16384,128]{1,0:T(8,128)} custom-call(s32[4096]{0:T(1024)} %agg_hbm.1, f32[4096,128]{1,0:T(8,128)} %bitcast.12), custom_call_target="tpu_custom_call" | custom-call | tf_op jit(solution)/shard_map/scatter/pallas_call | solution.py:282
  236.4 91.6 %coarse_leg.1 = f32[32,128,128]{2,1,0:T(8,128)S(1)} custom-call(s32[16,32]{1,0:T(8,128)} %bitcast.20, s32[32]{0:T(128)} %cnt_ref.3, f32[16384]{0:T(1024)} %diag_ref.1, f32[32,1,128]{2,1,0:T(1,128)} %bitcast.18, s32[4096]{0:T(1024)} %agg_hbm.1, s32[32768]{0:T(1024)} %bitcast.16, f32[16384,128]{1,0:T(8,128)} %scatter.1.coarse_hbm, ...), custom_call_target="tpu_custom_call" | custom-call | tf_op jit(solution)/shard_map/coarse_leg/pallas_call | solution.py:554
  327.9 1.3 copy.11

commit v6 on v5

--- a/solution.py
+++ b/solution.py
@@ -68,7 +68,7 @@
     return acc
 
 
-def stencil(w_ref, t_ref, col_ref, cnt_ref, hub_ref, rank_ref, hacc, finish, width=4):
+def stencil(w_ref, t_ref, col_ref, cnt_ref, hub_ref, rank_ref, hacc, finish, width=8):
     def hubs(i, _):
         for u in range(width):
             k = i * width + u
@@ -91,8 +91,8 @@
 
 def halo_kernel(
     col_ref, cnt_ref, lst_ref, guess_ref, rhs_ref, deg_ref, agg_ref, w_hbm,
-    x1_ref, res_ref, ids_ref,
-    w_ref, t1, t2, loc, sbuf, idbuf, hacc, hub_ref, rank_ref, wsem, ss, rs, idss, idrs,
+    x1_hbm, res_ref, ids_ref,
+    w_ref, x1_ref, t1, t2, loc, sbuf, idbuf, hacc, hub_ref, rank_ref, wsem, xsem, ss, rs, idss, idrs,
 ):
     spot = my_place()
     me = spot[0]
@@ -186,6 +186,8 @@
     for j in range(2):
         t2[NB + 2 * me + j] = loc[lst_ref[j, me]]
     send(ND - 1, t2, 1, place_id(*peer(ND - 1, spot)))
+    x1_copy = pltpu.make_async_copy(x1_ref, x1_hbm, xsem)
+    x1_copy.start()
     wait_all(1)
 
     def second(b, off):
@@ -193,6 +195,7 @@
         res_ref[b] = rhs_ref[b] - (deg * x1_ref[b] - off)
 
     stencil(w_ref, t2, col_ref, cnt_ref, hub_ref, rank_ref, hacc, second)
+    x1_copy.wait()
     pltpu.make_async_copy(ids_ref.at[pl.ds(0, 254)], ids_ref.at[pl.ds(0, 254)], idrs).wait()
     pltpu.make_async_copy(ids_ref.at[pl.ds(0, 254)], ids_ref.at[pl.ds(0, 254)], idss).wait()
 
@@ -208,9 +211,10 @@
             jax.ShapeDtypeStruct((2 * ND, 1, BS), jnp.int32),
         ),
         in_specs=[sm, sm, sm, vm, vm, vm, vm, pl.BlockSpec(memory_space=pl.ANY)],
-        out_specs=(vm, vm, vm),
+        out_specs=(pl.BlockSpec(memory_space=pltpu.HBM), vm, vm),
         scratch_shapes=[
             VMEM((NB, 16, BS, BS), bf16),
+            VMEM((NB, BS, BS), f32),
             VMEM((TB, BS, BS), bf16),
             VMEM((TB, BS, BS), bf16),
             VMEM((NB, BS, BS), bf16),
@@ -219,6 +223,7 @@
             VMEM((HUBS, BS, BS), f32),
             SMEM((HUBS,), jnp.int32),
             SMEM((NB,), jnp.int32),
+            pltpu.SemaphoreType.DMA,
             pltpu.SemaphoreType.DMA,
             pltpu.SemaphoreType.DMA((2,)),
             pltpu.SemaphoreType.DMA((2,)),

time: 330 us -> 332 us (level)
    pallas_call x1, Pallas kernels: 91.6 us -> 95.6 us  [coarse_leg(): pl.pallas_call(coarse_kernel, out_shape=VMEM((NB, BS, BS), f32), in_specs...]
where the time goes in v6:
time: 332 us
  Pallas kernels  330 us (99%)
    pallas_call x1, Pallas kernels, halo(): pl.pallas_call(halo_kernel, out_shape=(jax.ShapeDtypeStruct((NB, BS, BS),...  222 us
    pallas_call x1, Pallas kernels, coarse_leg(): pl.pallas_call(coarse_kernel, out_shape=VMEM((NB, BS, BS), f32), in_specs...  95.6 us
    pallas_call x1, Pallas kernels, scatter(): pl.pallas_call(scatter_kernel, out_shape=jax.ShapeDtypeStruct((NC, BS), f...  13.2 us

profile of v6, /device:TPU:0, one launch (start us, length us, event | category | flops | bytes accessed | tf_op | source)
XLA Modules:
  0.0 331.7 jit_solution(12379889350363275751)
XLA Ops:
  0.0 221.6 %halo.1 = (f32[32,128,128]{2,1,0:T(8,128)}, f32[32,128,128]{2,1,0:T(8,128)}, s32[256,1,128]{2,1,0:T(1,128)}) custom-call(s32[16,32]{1,0:T(8,128)} %bitcast.19, s32[32]{0:T(128)} %cnt_ref.3, s32[2,128]{1,0:T(2,128)} %bitcast.21, f32[32,128,128]{2,1,0:T(8,128)} %bitcast.13, f32[32,128,128]{2,1,0:T(8,128)} %bitcast.14, f32[32,1,128]{2,1,0:T(1,128)} %bitcast.17, ...), custom_call_target="tpu_custom_call" | custom-call | tf_op jit(solution)/shard_map/halo/pallas_call | solution.py:206
  221.6 13.2 %scatter.1.coarse_hbm = f32[16384,128]{1,0:T(8,128)} custom-call(s32[4096]{0:T(1024)} %agg_hbm.1, f32[4096,128]{1,0:T(8,128)} %bitcast.12), custom_call_target="tpu_custom_call" | custom-call | tf_op jit(solution)/shard_map/scatter/pallas_call | solution.py:287
  234.8 95.6 %coarse_leg.1 = f32[32,128,128]{2,1,0:T(8,128)S(1)} custom-call(s32[16,32]{1,0:T(8,128)} %bitcast.20, s32[32]{0:T(128)} %cnt_ref.3, f32[16384]{0:T(1024)} %diag_ref.1, f32[32,1,128]{2,1,0:T(1,128)} %bitcast.18, s32[4096]{0:T(1024)} %agg_hbm.1, s32[32768]{0:T(1024)} %bitcast.16, f32[16384,128]{1,0:T(8,128)} %scatter.1.coarse_hbm, ...), custom_call_target="tpu_custom_call" | custom-call | tf_op jit(solution)/shard_map/coarse_leg/pallas_call | solution.py:559
  330.4 1.3 copy.11
